TPU v7x, 64 devices: a 2x2x8 block of a 4x4x8 slice. The times are simulated.
64 devices in a mesh: graph: 4 (over x, y), nodes: 16 (over z, core).
Axes of the slice: x: 2, y: 2, z: 8, core: 2. Of those that a mesh axis runs over, the one named last changes fastest.
The devices are a block of a 4x4x8 slice.
Arguments:
- node_feats: bfloat16 [131072, 200], P(('graph', 'nodes')), parts along dimension 0
- a_int: bfloat16 [131072, 2048], P(('graph', 'nodes')), parts along dimension 0
- a_halo: bfloat16 [131072, 1024], P(('graph', 'nodes')), parts along dimension 0
- send_idx: int32 [256, 256], P(('graph', 'nodes')), parts along dimension 0
- w_first: bfloat16 [200, 512], replicated
- w_second: bfloat16 [512, 107], replicated
- grad_out: bfloat16 [131072, 107], P(('graph', 'nodes')), parts along dimension 0
Outputs:
- output 1: float32 [800, 512], P('graph'), parts along dimension 0
- output 2: float32 [2048, 107], P('graph'), parts along dimension 0
- output 3: float32 [131072, 200], P(('graph', 'nodes')), parts along dimension 0
There are 4 independent parts. A program takes and returns all parts, laid end to end along the dimension named above; an argument that names none is the same for every part.
All inputs are finite; a program needn't handle non-finite values.
Results may differ from a plain program's by a relative error of at most 0.00607032.
Values are sent between devices in bfloat16 or wider.
A program may use at most 768 MiB of HBM per device.

v0:
```python
import jax
import jax.numpy as jnp
from jax import lax
from jax.sharding import PartitionSpec as P


def link_offsets(num_links):
    return [(link // 2 + 1) * (1 - 2 * (link % 2)) for link in range(num_links)]


def shift_pairs(axis_size, offset):
    return [(source, (source + offset) % axis_size) for source in range(axis_size)]


def contract_rows(left_rows, right_rows):
    return lax.dot_general(left_rows, right_rows, (((0,), (0,)), ((), ())), preferred_element_type=jnp.float32)


def halo_rows(features, send_idx, axis_size):
    sent_rows = jnp.take(features, send_idx, axis=0)
    received = [lax.ppermute(sent_rows[link], "nodes", shift_pairs(axis_size, offset)) for link, offset in enumerate(link_offsets(send_idx.shape[0]))]
    return jnp.concatenate(received, axis=0)


def aggregate(a_int, a_halo, features, send_idx, axis_size):
    remote = halo_rows(features, send_idx, axis_size)
    return jnp.dot(a_int, features, preferred_element_type=jnp.float32) + jnp.dot(a_halo, remote, preferred_element_type=jnp.float32)


def aggregate_back(a_int, a_halo, grad_rows, send_idx, axis_size):
    num_slots = send_idx.shape[1]
    inner_sum = contract_rows(a_int, grad_rows)
    outward = contract_rows(a_halo, grad_rows).astype(jnp.bfloat16)
    received = [lax.ppermute(outward[link * num_slots:(link + 1) * num_slots], "nodes", shift_pairs(axis_size, -offset)) for link, offset in enumerate(link_offsets(send_idx.shape[0]))]
    returned = jnp.concatenate(received, axis=0).astype(jnp.float32)
    return inner_sum.at[send_idx.reshape(-1)].add(returned)


def solution(mesh):
    axis_size = mesh.shape["nodes"]
    row_spec = P(("graph", "nodes"), None)
    replicated = P(None, None)
    part_spec = P("graph", None)

    def device_step(node_feats, a_int, a_halo, send_idx, w_first, w_second, grad_out):
        z_first = aggregate(a_int, a_halo, node_feats, send_idx, axis_size).astype(jnp.bfloat16)
        hidden = jnp.maximum(jnp.dot(z_first, w_first, preferred_element_type=jnp.float32), 0.0).astype(jnp.bfloat16)
        z_second = aggregate(a_int, a_halo, hidden, send_idx, axis_size).astype(jnp.bfloat16)
        dw_second = lax.psum(contract_rows(z_second, grad_out), "nodes")
        dz_second = lax.dot_general(grad_out, w_second, (((1,), (1,)), ((), ())), preferred_element_type=jnp.float32).astype(jnp.bfloat16)
        d_hidden = aggregate_back(a_int, a_halo, dz_second, send_idx, axis_size)
        grad_pre = jnp.where(hidden > 0, d_hidden, 0.0).astype(jnp.bfloat16)
        dw_first = lax.psum(contract_rows(z_first, grad_pre), "nodes")
        dz_first = lax.dot_general(grad_pre, w_first, (((1,), (1,)), ((), ())), preferred_element_type=jnp.float32).astype(jnp.bfloat16)
        grad_feats = aggregate_back(a_int, a_halo, dz_first, send_idx, axis_size)
        return dw_first, dw_second, grad_feats

    return jax.shard_map(device_step, mesh=mesh, in_specs=(row_spec, row_spec, row_spec, row_spec, replicated, replicated, row_spec), out_specs=(part_spec, part_spec, row_spec), check_vma=False)
```

profile of v0, /device:TPU:21, one launch (start us, length us, event | category | flops | bytes accessed | tf_op | source)
XLA Modules:
  0.0 224.2 jit_solution(8853858623810234276)
XLA Ops:
  7.3 0.7 fusion.26
  8.0 0.7 compare_and_fusion
  8.7 1.4 copy.10
  10.2 3.9 %gather_fusion = bf16[1024,200]{1,0:T(8,128)(2,1)S(1)} fusion(bf16[2048,200]{1,0:T(8,128)(2,1)S(1)} %copy.10, s32[1024]{0:T(1024)S(1)} %broadcast_clamp_fusion), kind=kCustom, calls=%fused_computation | custom fusion | bytes 823296 | tf_op jit(solution)/shard_map/jit(_take)/gather | solution.py:20
  14.1 0.2 broadcast_select_fusion.1
  14.4 7.9 %collective-permute-start.3 = (bf16[256,200]{1,0:T(8,128)(2,1)S(1)}, bf16[256,200]{1,0:T(8,128)(2,1)S(1)}, u32[]{:S(2)}, u32[]{:S(2)}) collective-permute-start(bf16[256,200]{1,0:T(8,128)(2,1)S(1)} %get-tuple-element.17), channel_id=1, source_target_pairs={{0,14},{1,15},{2,0},{3,1},{4,2},{5,3},{6,4},{7,5},{8,6},{9,7},{10,... | collective-permute-start | bytes 307208 | tf_op jit(solution)/shard_map/ppermute | solution.py:21
  22.3 0.9 collective-permute-start.1
  23.2 0.9 collective-permute-start
  24.1 0.7 convolution_convert_fusion
  24.8 2.3 %fusion.2 = bf16[1024,512]{0,1:T(8,128)(2,1)S(1)} fusion(bf16[2048,512]{1,0:T(8,128)(2,1)S(1)} %convolution_convert_fusion, bf16[2048,1024]{1,0:T(8,128)(2,1)S(1)} %copy-done.2), kind=kOutput, calls=%fused_computation.15 | convolution fusion | flops 2148007936 | bytes 7340032 | tf_op jit(solution)/shard_map/dot_general | solution.py:16
  27.2 1.0 fusion.31
  28.2 0.6 copy-done.4
  28.8 2.8 %fusion.33 = f32[2048,200]{0,1:T(8,128)S(1)} fusion(bf16[2048,2048]{1,0:T(8,128)(2,1)S(1)} %bitcast.69, bf16[2048,200]{0,1:T(8,128)(2,1)S(1)} %copy-done.4), kind=kOutput, calls=%fused_computation.55 | convolution fusion | flops 1677721600 | bytes 10846208 | tf_op jit(solution)/shard_map/dot_general | solution.py:27
  31.7 6.2 %convolution_bitcast_fusion = f32[2048,512]{0,1:T(8,128)} fusion(bf16[2048,512]{1,0:T(8,128)(2,1)S(1)} %convolution_convert_fusion, bf16[2048,2048]{1,0:T(8,128)(2,1)S(1)} %bitcast.69), kind=kOutput, calls=%fused_computation.7 | convolution fusion | flops 4294967296 | bytes 14680064 | tf_op jit(solution)/shard_map/dot_general | solution.py:16
  37.9 5.4 %copy.11 = f32[2048,512]{1,0:T(8,128)} copy(f32[2048,512]{0,1:T(8,128)} %convolution_bitcast_fusion) | data formatting | bytes 8388608 | tf_op jit(solution)/shard_map/dot_general | solution.py:16
  43.3 3.9 %collective-permute-start.6 = (bf16[256,512]{0,1:T(8,128)(2,1)}, bf16[256,512]{0,1:T(8,128)(2,1)}, u32[]{:S(2)}, u32[]{:S(2)}) collective-permute-start(bf16[256,512]{0,1:T(8,128)(2,1)} %get-tuple-element.14), channel_id=1, source_target_pairs={{0,14},{1,15},{2,0},{3,1},{4,2},{5,3},{6,4},{7,5},{8,6},{9,7},{10,... | collective-permute-start | bytes 786440 | tf_op jit(solution)/shard_map/ppermute | solution.py:34
  47.2 0.5 collective-permute-start.4
  47.7 3.7 %fusion.1 = bf16[2048,200]{0,1:T(8,128)(2,1)S(1)} fusion(f32[2048,200]{0,1:T(8,128)S(1)} %fusion.33, bf16[2048,1024]{1,0:T(8,128)(2,1)} %param.9, bf16[256,200]{1,0:T(8,128)(2,1)S(1)} %collective-permute-done.3, bf16[256,200]{1,0:T(8,128)(2,1)S(1)} %collective-permute-done.2, bf16[256,200]{1,0:T(8,128)(2,1)S(1)} %collective-permute-done.1, ...), kind=kOutput, calls=%fused_computation.12 | convolution fusion | flops 841318400 | bytes 7061504 | tf_op jit(solution)/shard_map/dot_general | solution.py:27
  51.5 0.8 maximum_convert_fusion
  52.2 9.6 %fusion.34 = f32[512,2048]{1,0:T(8,128)} fusion(bf16[2048,512]{1,0:T(8,128)(2,1)S(1)} %maximum_convert_fusion, bf16[2048,2048]{1,0:T(8,128)(2,1)} %param.8), kind=kOutput, calls=%fused_computation.56 | convolution fusion | flops 4294967296 | bytes 14680064 | tf_op jit(solution)/shard_map/dot_general | solution.py:27
  61.9 5.1 %gather_fusion.1 = bf16[1024,512]{1,0:T(8,128)(2,1)} fusion(bf16[2048,512]{1,0:T(8,128)(2,1)S(1)} %maximum_convert_fusion, s32[1024]{0:T(1024)S(1)} %broadcast_clamp_fusion), kind=kCustom, calls=%fused_computation.1 | custom fusion | bytes 2101248 | tf_op jit(solution)/shard_map/jit(_take)/gather | solution.py:20
  67.0 1.4 broadcast_select_fusion
  68.4 1.0 slice_bitcast_fusion.3
  69.4 2.2 collective-permute-start.11
  71.6 2.4 %collective-permute-start.9 = (bf16[256,512]{1,0:T(8,128)(2,1)}, bf16[256,512]{1,0:T(8,128)(2,1)}, u32[]{:S(2)}, u32[]{:S(2)}) collective-permute-start(bf16[256,512]{1,0:T(8,128)(2,1)} %get-tuple-element.11), channel_id=1, source_target_pairs={{0,15},{1,0},{2,1},{3,2},{4,3},{5,4},{6,5},{7,6},{8,7},{9,8},{10,9... | collective-permute-start | bytes 786440 | tf_op jit(solution)/shard_map/ppermute | solution.py:21
  74.0 2.8 %maximum_convert_fusion.1 = f32[1024,512]{0,1:T(8,128)} fusion(bf16[256,512]{0,1:T(8,128)(2,1)} %collective-permute-done.7, bf16[256,512]{0,1:T(8,128)(2,1)} %collective-permute-done.6, bf16[256,512]{0,1:T(8,128)(2,1)} %collective-permute-done.5, bf16[256,512]{0,1:T(8,128)(2,1)} %collective-permute-done.4), kind=kLoop, calls=%fused_computation.19 | loop fusion | flops 4194304 | bytes 3145728 | tf_op jit(solution)/shard_map/convert_element_type | solution.py:35
  76.8 2.9 %copy.12 = f32[1024,512]{1,0:T(8,128)} copy(f32[1024,512]{0,1:T(8,128)} %maximum_convert_fusion.1) | data formatting | bytes 4194304 | tf_op jit(solution)/shard_map/convert_element_type | solution.py:35
  79.7 11.6 %scatter_fusion = f32[2048,512]{1,0:T(8,128)} fusion(f32[2048,512]{1,0:T(8,128)} %copy.11, s32[1024]{0:T(1024)S(1)} %bitcast.63, f32[1024,512]{1,0:T(8,128)} %copy.12), kind=kCustom, calls=%fused_computation.2 | custom fusion | flops 524288 | bytes 6295552 | tf_op jit(solution)/shard_map/scatter-add | solution.py:36
  91.3 3.2 %convolution_convert_fusion.1 = bf16[2048,200]{0,1:T(8,128)(2,1)S(1)} fusion(bf16[200,512]{1,0:T(8,128)(2,1)} %param.11, f32[2048,512]{1,0:T(8,128)} %scatter_fusion, bf16[2048,512]{1,0:T(8,128)(2,1)S(1)} %maximum_convert_fusion), kind=kOutput, calls=%fused_computation.13 | convolution fusion | flops 424034304 | bytes 7315456 | tf_op jit(solution)/shard_map/dot_general | solution.py:54
  94.5 0.3 copy-done.3
  94.8 1.1 fusion.3
  95.9 0.8 fusion.32
  96.7 0.7 copy-done.1
  97.4 1.5 fusion.30
  98.9 3.5 %collective-permute-start.14 = (bf16[256,200]{0,1:T(8,128)(2,1)}, bf16[256,200]{0,1:T(8,128)(2,1)S(1)}, u32[]{:S(2)}, u32[]{:S(2)}) collective-permute-start(bf16[256,200]{0,1:T(8,128)(2,1)} %get-tuple-element.22), channel_id=1, source_target_pairs={{0,14},{1,15},{2,0},{3,1},{4,2},{5,3},{6,4},{7,5},{8,6},{9,7},{10,... | collective-permute-start | bytes 307208 | tf_op jit(solution)/shard_map/ppermute | solution.py:34
  102.5 0.5 collective-permute-start.12
  103.0 7.5 %fusion.4 = f32[512,107]{0,1:T(8,128)} fusion(bf16[2048,107]{0,1:T(8,128)(2,1)S(1)} %copy-done, f32[512,2048]{1,0:T(8,128)} %fusion.34, bf16[2048,1024]{1,0:T(8,128)(2,1)} %param.9, bf16[256,512]{1,0:T(8,128)(2,1)} %collective-permute-done.11, bf16[256,512]{1,0:T(8,128)(2,1)} %collective-permute-done.10, bf16[256,512]{1,0:T(8,128)(2,1)} %collective-permute-done.9, ...), kind=kOutput, calls=%fused_computation.18 | convolution fusion | flops 2378170368 | bytes 10094592 | tf_op jit(solution)/shard_map/dot_general | solution.py:16
  110.5 6.4 %convolution_bitcast_fusion.1 = f32[2048,200]{0,1:T(8,128)} fusion(bf16[2048,200]{0,1:T(8,128)(2,1)S(1)} %copy-done.6, bf16[2048,2048]{1,0:T(8,128)(2,1)} %param.8), kind=kOutput, calls=%fused_computation.9 | convolution fusion | flops 1677721600 | bytes 10846208 | tf_op jit(solution)/shard_map/dot_general | solution.py:16
  116.9 1.8 copy.13
  118.8 0.6 copy-done.9
  119.4 0.6 copy-done.10
  120.1 1.1 maximum_convert_fusion.2
  121.2 1.3 copy.14
  122.5 7.5 %scatter_fusion.1 = f32[2048,200]{1,0:T(8,128)S(1)} fusion(f32[2048,200]{1,0:T(8,128)S(1)} %copy.13, s32[1024]{0:T(1024)S(1)} %bitcast.64, f32[1024,200]{1,0:T(8,128)} %copy.14), kind=kCustom, calls=%fused_computation.3 | custom fusion | flops 204800 | bytes 2461696 | tf_op jit(solution)/shard_map/scatter-add | solution.py:36
  130.1 1.7 copy.15
  131.8 82.1 %all-reduce.3.cloned.1.call-done = (f32[200,512]{1,0:T(8,128)}, f32[512,107]{0,1:T(8,128)}) async-done(((f32[200,512]{1,0:T(8,128)}, f32[512,107]{0,1:T(8,128)}), (f32[200,512]{1,0:T(8,128)}, f32[512,107]{0,1:T(8,128)})) %all-reduce.3.cloned.1.call-update) | async-done | bytes 628752 | tf_op jit(solution)/shard_map/psum | solution.py:53
  213.9 1.8 copy.22
  215.7 1.6 copy.23
  (54 shorter events, 0.3 us)
Async XLA Ops:
  7.2 16.9 %copy-start = (bf16[2048,107]{0,1:T(8,128)(2,1)S(1)}, bf16[2048,107]{0,1:T(8,128)(2,1)}, u32[]{:S(2)}) copy-start(bf16[2048,107]{0,1:T(8,128)(2,1)} %param.13) | copy-start | bytes 1314820
  7.2 206.7 %all-reduce.3.cloned.1.call-start = ((), (), s32[]{:S(2)}) async-start(), calls=%async_computation | async-start | bytes 1277952 | tf_op jit(solution)/shard_map/psum | solution.py:53
  14.1 9.9 %copy-start.8 = (bf16[512,107]{0,1:T(8,128)(2,1)S(1)}, bf16[512,107]{0,1:T(8,128)(2,1)}, u32[]{:S(2)}) copy-start(bf16[512,107]{0,1:T(8,128)(2,1)} %param.12) | copy-start | bytes 328708
  14.1 10.7 %copy-start.2 = (bf16[2048,1024]{1,0:T(8,128)(2,1)S(1)}, bf16[2048,1024]{1,0:T(8,128)(2,1)}, u32[]{:S(2)}) copy-start(bf16[2048,1024]{1,0:T(8,128)(2,1)} %param.9) | copy-start | bytes 12582916
  14.4 28.9 %collective-permute-start.3 = (bf16[256,200]{1,0:T(8,128)(2,1)S(1)}, bf16[256,200]{1,0:T(8,128)(2,1)S(1)}, u32[]{:S(2)}, u32[]{:S(2)}) collective-permute-start(bf16[256,200]{1,0:T(8,128)(2,1)S(1)} %get-tuple-element.17), channel_id=1, source_target_pairs={{0,14},{1,15},{2,0},{3,1},{4,2},{5,3},{6,4},{7,5},{8,6},{9,7},{10,... | collective-permute-start | bytes 307208 | tf_op jit(solution)/shard_map/ppermute | solution.py:21
  22.3 24.9 %collective-permute-start.2 = (bf16[256,200]{1,0:T(8,128)(2,1)S(1)}, bf16[256,200]{1,0:T(8,128)(2,1)S(1)}, u32[]{:S(2)}, u32[]{:S(2)}) collective-permute-start(bf16[256,200]{1,0:T(8,128)(2,1)S(1)} %get-tuple-element.18), channel_id=1, source_target_pairs={{0,2},{1,3},{2,4},{3,5},{4,6},{5,7},{6,8},{7,9},{8,10},{9,11},{10,... | collective-permute-start | bytes 307208 | tf_op jit(solution)/shard_map/ppermute | solution.py:21
  22.3 24.9 %collective-permute-start.1 = (bf16[256,200]{1,0:T(8,128)(2,1)S(1)}, bf16[256,200]{1,0:T(8,128)(2,1)S(1)}, u32[]{:S(2)}, u32[]{:S(2)}) collective-permute-start(bf16[256,200]{1,0:T(8,128)(2,1)S(1)} %get-tuple-element.19), channel_id=1, source_target_pairs={{0,15},{1,0},{2,1},{3,2},{4,3},{5,4},{6,5},{7,6},{8,7},{9,8},{10,9... | collective-permute-start | bytes 307208 | tf_op jit(solution)/shard_map/ppermute | solution.py:21
  23.2 24.5 %collective-permute-start = (bf16[256,200]{1,0:T(8,128)(2,1)S(1)}, bf16[256,200]{1,0:T(8,128)(2,1)S(1)}, u32[]{:S(2)}, u32[]{:S(2)}) collective-permute-start(bf16[256,200]{1,0:T(8,128)(2,1)S(1)} %get-tuple-element.16), channel_id=1, source_target_pairs={{0,1},{1,2},{2,3},{3,4},{4,5},{5,6},{6,7},{7,8},{8,9},{9,10},{10,1... | collective-permute-start | bytes 307208 | tf_op jit(solution)/shard_map/ppermute | solution.py:21
  24.1 4.1 %slice-start = ((s8[8388608]{0:T(1024)(128)(4,1)}), s8[4194304]{0:T(1024)(128)(4,1)S(1)}, s32[]{:S(2)}) async-start(s8[8388608]{0:T(1024)(128)(4,1)} %bitcast.68), calls=%async_computation.1 | async-start | bytes 8388608
  24.8 3.4 %slice-start.1 = ((s8[8388608]{0:T(1024)(128)(4,1)}), s8[4194304]{0:T(1024)(128)(4,1)S(1)}, s32[]{:S(2)}) async-start(s8[8388608]{0:T(1024)(128)(4,1)} %bitcast.68), calls=%async_computation.2 | async-start | bytes 8388608
  27.2 1.7 copy-start.4
  28.2 43.4 %collective-permute-start.7 = (bf16[256,512]{0,1:T(8,128)(2,1)}, bf16[256,512]{0,1:T(8,128)(2,1)}, u32[]{:S(2)}, u32[]{:S(2)}) collective-permute-start(bf16[256,512]{0,1:T(8,128)(2,1)} %get-tuple-element.13), channel_id=1, source_target_pairs={{0,2},{1,3},{2,4},{3,5},{4,6},{5,7},{6,8},{7,9},{8,10},{9,11},{10,... | collective-permute-start | bytes 786440 | tf_op jit(solution)/shard_map/ppermute | solution.py:34
  31.7 6.2 %copy-start.11 = (s32[4,256]{1,0:T(4,128)S(1)}, s32[4,256]{1,0:T(4,128)}, u32[]{:S(2)}) copy-start(s32[4,256]{1,0:T(4,128)} %param.10) | copy-start | bytes 12292
  43.3 28.3 %collective-permute-start.6 = (bf16[256,512]{0,1:T(8,128)(2,1)}, bf16[256,512]{0,1:T(8,128)(2,1)}, u32[]{:S(2)}, u32[]{:S(2)}) collective-permute-start(bf16[256,512]{0,1:T(8,128)(2,1)} %get-tuple-element.14), channel_id=1, source_target_pairs={{0,14},{1,15},{2,0},{3,1},{4,2},{5,3},{6,4},{7,5},{8,6},{9,7},{10,... | collective-permute-start | bytes 786440 | tf_op jit(solution)/shard_map/ppermute | solution.py:34
  47.2 26.7 %collective-permute-start.5 = (bf16[256,512]{0,1:T(8,128)(2,1)}, bf16[256,512]{0,1:T(8,128)(2,1)}, u32[]{:S(2)}, u32[]{:S(2)}) collective-permute-start(bf16[256,512]{0,1:T(8,128)(2,1)} %get-tuple-element.15), channel_id=1, source_target_pairs={{0,1},{1,2},{2,3},{3,4},{4,5},{5,6},{6,7},{7,8},{8,9},{9,10},{10,1... | collective-permute-start | bytes 786440 | tf_op jit(solution)/shard_map/ppermute | solution.py:34
  47.2 4.2 %copy-start.7 = (bf16[200,512]{1,0:T(8,128)(2,1)S(1)}, bf16[200,512]{1,0:T(8,128)(2,1)}, u32[]{:S(2)}) copy-start(bf16[200,512]{1,0:T(8,128)(2,1)} %param.11) | copy-start | bytes 614404
  47.2 26.7 %collective-permute-start.4 = (bf16[256,512]{0,1:T(8,128)(2,1)}, bf16[256,512]{0,1:T(8,128)(2,1)}, u32[]{:S(2)}, u32[]{:S(2)}) collective-permute-start(bf16[256,512]{0,1:T(8,128)(2,1)} %get-tuple-element.12), channel_id=1, source_target_pairs={{0,15},{1,0},{2,1},{3,2},{4,3},{5,4},{6,5},{7,6},{8,7},{9,8},{10,9... | collective-permute-start | bytes 786440 | tf_op jit(solution)/shard_map/ppermute | solution.py:34
  69.4 29.5 %collective-permute-start.11 = (bf16[256,512]{1,0:T(8,128)(2,1)}, bf16[256,512]{1,0:T(8,128)(2,1)}, u32[]{:S(2)}, u32[]{:S(2)}) collective-permute-start(bf16[256,512]{1,0:T(8,128)(2,1)} %get-tuple-element.9), channel_id=1, source_target_pairs={{0,14},{1,15},{2,0},{3,1},{4,2},{5,3},{6,4},{7,5},{8,6},{9,7},{10,... | collective-permute-start | bytes 786440 | tf_op jit(solution)/shard_map/ppermute | solution.py:21
  71.6 30.9 %collective-permute-start.10 = (bf16[256,512]{1,0:T(8,128)(2,1)}, bf16[256,512]{1,0:T(8,128)(2,1)}, u32[]{:S(2)}, u32[]{:S(2)}) collective-permute-start(bf16[256,512]{1,0:T(8,128)(2,1)} %get-tuple-element.10), channel_id=1, source_target_pairs={{0,2},{1,3},{2,4},{3,5},{4,6},{5,7},{6,8},{7,9},{8,10},{9,11},{10,... | collective-permute-start | bytes 786440 | tf_op jit(solution)/shard_map/ppermute | solution.py:21
  71.6 30.9 %collective-permute-start.9 = (bf16[256,512]{1,0:T(8,128)(2,1)}, bf16[256,512]{1,0:T(8,128)(2,1)}, u32[]{:S(2)}, u32[]{:S(2)}) collective-permute-start(bf16[256,512]{1,0:T(8,128)(2,1)} %get-tuple-element.11), channel_id=1, source_target_pairs={{0,15},{1,0},{2,1},{3,2},{4,3},{5,4},{6,5},{7,6},{8,7},{9,8},{10,9... | collective-permute-start | bytes 786440 | tf_op jit(solution)/shard_map/ppermute | solution.py:21
  74.0 29.0 %collective-permute-start.8 = (bf16[256,512]{1,0:T(8,128)(2,1)}, bf16[256,512]{1,0:T(8,128)(2,1)}, u32[]{:S(2)}, u32[]{:S(2)}) collective-permute-start(bf16[256,512]{1,0:T(8,128)(2,1)} %get-tuple-element.8), channel_id=1, source_target_pairs={{0,1},{1,2},{2,3},{3,4},{4,5},{5,6},{6,7},{7,8},{8,9},{9,10},{10,1... | collective-permute-start | bytes 786440 | tf_op jit(solution)/shard_map/ppermute | solution.py:21
  91.3 3.5 %copy-start.3 = (bf16[2048,1024]{1,0:T(8,128)(2,1)S(1)}, bf16[2048,1024]{1,0:T(8,128)(2,1)}, u32[]{:S(2)}) copy-start(bf16[2048,1024]{1,0:T(8,128)(2,1)} %param.9) | copy-start | bytes 12582916
  94.8 1.1 copy-start.5
  94.8 2.6 %copy-start.1 = (f32[2048,512]{1,0:T(8,128)S(1)}, f32[2048,512]{1,0:T(8,128)}, u32[]{:S(2)}) copy-start(f32[2048,512]{1,0:T(8,128)} %scatter_fusion) | copy-start | bytes 12582916
  96.6 22.1 %collective-permute-start.15 = (bf16[256,200]{0,1:T(8,128)(2,1)}, bf16[256,200]{0,1:T(8,128)(2,1)}, u32[]{:S(2)}, u32[]{:S(2)}) collective-permute-start(bf16[256,200]{0,1:T(8,128)(2,1)} %get-tuple-element.21), channel_id=1, source_target_pairs={{0,2},{1,3},{2,4},{3,5},{4,6},{5,7},{6,8},{7,9},{8,10},{9,11},{10,... | collective-permute-start | bytes 307208 | tf_op jit(solution)/shard_map/ppermute | solution.py:34
  98.9 19.9 %collective-permute-start.14 = (bf16[256,200]{0,1:T(8,128)(2,1)}, bf16[256,200]{0,1:T(8,128)(2,1)S(1)}, u32[]{:S(2)}, u32[]{:S(2)}) collective-permute-start(bf16[256,200]{0,1:T(8,128)(2,1)} %get-tuple-element.22), channel_id=1, source_target_pairs={{0,14},{1,15},{2,0},{3,1},{4,2},{5,3},{6,4},{7,5},{8,6},{9,7},{10,... | collective-permute-start | bytes 307208 | tf_op jit(solution)/shard_map/ppermute | solution.py:34
  102.4 16.4 %collective-permute-start.13 = (bf16[256,200]{0,1:T(8,128)(2,1)}, bf16[256,200]{0,1:T(8,128)(2,1)S(1)}, u32[]{:S(2)}, u32[]{:S(2)}) collective-permute-start(bf16[256,200]{0,1:T(8,128)(2,1)} %get-tuple-element.23), channel_id=1, source_target_pairs={{0,1},{1,2},{2,3},{3,4},{4,5},{5,6},{6,7},{7,8},{8,9},{9,10},{10,1... | collective-permute-start | bytes 307208 | tf_op jit(solution)/shard_map/ppermute | solution.py:34
  102.5 8.0 %copy-start.6 = (bf16[2048,200]{0,1:T(8,128)(2,1)S(1)}, bf16[2048,200]{0,1:T(8,128)(2,1)}, u32[]{:S(2)}) copy-start(bf16[2048,200]{0,1:T(8,128)(2,1)} %copy-done.5) | copy-start | bytes 2457604
  102.5 17.6 %collective-permute-start.12 = (bf16[256,200]{0,1:T(8,128)(2,1)S(1)}, bf16[256,200]{0,1:T(8,128)(2,1)}, u32[]{:S(2)}, u32[]{:S(2)}) collective-permute-start(bf16[256,200]{0,1:T(8,128)(2,1)S(1)} %get-tuple-element.20), channel_id=1, source_target_pairs={{0,15},{1,0},{2,1},{3,2},{4,3},{5,4},{6,5},{7,6},{8,7},{9,8},{10,9... | collective-permute-start | bytes 307208 | tf_op jit(solution)/shard_map/ppermute | solution.py:34
  118.8 0.6 copy-start.9
  119.4 0.6 copy-start.10
Sparse Core Ops, SparseCore 0:
  110.6 103.2 all-reduce.2
where the time goes:
time: 225 us; the launch traced here: 224 us
  waiting for transfers between devices  82.2 us (37%)
  matrix products  45.8 us (20%)
  local copies, waits for them, and re-layouts  32.9 us (15%)
  other arithmetic  26.1 us (12%)
  starting transfers between devices  22.7 us (10%)
  between operations  14.4 us (6%)
    psum x1, waiting for transfers between devices, device_step(): dw_first = lax.psum(contract_rows(z_first, grad_pre), 'nodes')  82.1 us
    dot_general x6, matrix products, contract_rows(): lax.dot_general(left_rows, right_rows, (((0,), (0,)), ((), ())), preferre...  25 us
    scatter-add x2, other arithmetic, aggregate_back(): return inner_sum.at[send_idx.reshape(-1)].add(returned)  19.1 us
    ppermute x8, starting transfers between devices, halo_rows(): lax.ppermute(sent_rows[link], 'nodes', shift_pairs(axis_size, offset))  14.2 us
    dot_general x2, matrix products, aggregate(): jnp.dot(a_int, features, preferred_element_type=jnp.float32)  12.5 us
    unnamed x34, local copies, waits for them, and re-layouts  9.57 us
    gather x2, local copies, waits for them, and re-layouts, halo_rows(): sent_rows = jnp.take(features, send_idx, axis=0)  9.02 us
    ppermute x8, starting transfers between devices, aggregate_back(): lax.ppermute(outward[link * num_slots:(link + 1) * num_slots], 'nodes', s...  8.45 us
  transfers between devices with their start and end apart: 17, of which 1 were waited for; matrix products, arithmetic and copies ran while one was open for 41% of the time, Pallas kernels for 0%

commit v1 on v0

--- a/solution.py
+++ b/solution.py
@@ -43,12 +43,17 @@
     part_spec = P("graph", None)
 
     def device_step(node_feats, a_int, a_halo, send_idx, w_first, w_second, grad_out):
+        classes = grad_out.shape[1]
+        pulled = aggregate_back(a_int, a_halo, grad_out, send_idx, axis_size)
+        pulled_high = pulled.astype(jnp.bfloat16)
+        pulled_low = (pulled - pulled_high.astype(jnp.float32)).astype(jnp.bfloat16)
+        pulled_pair = jnp.concatenate([pulled_high, pulled_low], axis=1)
+        w_pair = jnp.concatenate([w_second, w_second], axis=1)
         z_first = aggregate(a_int, a_halo, node_feats, send_idx, axis_size).astype(jnp.bfloat16)
         hidden = jnp.maximum(jnp.dot(z_first, w_first, preferred_element_type=jnp.float32), 0.0).astype(jnp.bfloat16)
-        z_second = aggregate(a_int, a_halo, hidden, send_idx, axis_size).astype(jnp.bfloat16)
-        dw_second = lax.psum(contract_rows(z_second, grad_out), "nodes")
-        dz_second = lax.dot_general(grad_out, w_second, (((1,), (1,)), ((), ())), preferred_element_type=jnp.float32).astype(jnp.bfloat16)
-        d_hidden = aggregate_back(a_int, a_halo, dz_second, send_idx, axis_size)
+        second_pair = contract_rows(hidden, pulled_pair)
+        dw_second = lax.psum(second_pair[:, :classes] + second_pair[:, classes:], "nodes")
+        d_hidden = lax.dot_general(pulled_pair, w_pair, (((1,), (1,)), ((), ())), preferred_element_type=jnp.float32)
         grad_pre = jnp.where(hidden > 0, d_hidden, 0.0).astype(jnp.bfloat16)
         dw_first = lax.psum(contract_rows(z_first, grad_pre), "nodes")
         dz_first = lax.dot_general(grad_pre, w_first, (((1,), (1,)), ((), ())), preferred_element_type=jnp.float32).astype(jnp.bfloat16)

time: 225 us -> 188 us (0.84)
  local copies, waits for them, and re-layouts: 32.9 us -> 17.1 us
  matrix products: 45.8 us -> 34.5 us
  other arithmetic: 26.1 us -> 17.3 us
  starting transfers between devices: 22.7 us -> 20.3 us
    ppermute x8 -> x4, starting transfers between devices: 14.2 us -> 5.1 us  [halo_rows(): lax.ppermute(sent_rows[link], 'nodes', shift_pairs(axis_size, offset))]
    ppermute x8, starting transfers between devices: 8.45 us -> 15.2 us  [aggregate_back(): lax.ppermute(outward[link * num_slots:(link + 1) * num_slots], 'nodes', s...]
    dot_general x2 -> x1, local copies, waits for them, and re-layouts: 7.29 us -> 1.84 us  [contract_rows(): lax.dot_general(left_rows, right_rows, (((0,), (0,)), ((), ())), preferre...]
    dot_general x2 -> x1, matrix products: 12.5 us -> 7.39 us  [aggregate(): jnp.dot(a_int, features, preferred_element_type=jnp.float32)]
    gather x2 -> x1, local copies, waits for them, and re-layouts: 9.02 us -> 3.94 us  [halo_rows(): sent_rows = jnp.take(features, send_idx, axis=0)]
    scatter-add x2, other arithmetic: 19.1 us -> 14.2 us  [aggregate_back(): return inner_sum.at[send_idx.reshape(-1)].add(returned)]
    dot_general x6, matrix products: 25 us -> 20.7 us  [contract_rows(): lax.dot_general(left_rows, right_rows, (((0,), (0,)), ((), ())), preferre...]
    convert_element_type x2, local copies, waits for them, and re-layouts: 4.24 us -> 1.51 us  [aggregate_back(): returned = jnp.concatenate(received, axis=0).astype(jnp.float32)]
  transfers between devices with their start and end apart: 17 -> 13, of which waited for: 1 -> 1; matrix products, arithmetic and copies ran while one was open for 41% -> 25% of each run, Pallas kernels for 0% -> 0%
where the time goes in v1:
time: 188 us
  waiting for transfers between devices  84.4 us (45%)
  matrix products  34.5 us (18%)
  starting transfers between devices  20.3 us (11%)
  other arithmetic  17.3 us (9%)
  local copies, waits for them, and re-layouts  17.1 us (9%)
  between operations  14.4 us (8%)
    psum x1, waiting for transfers between devices, device_step(): dw_first = lax.psum(contract_rows(z_first, grad_pre), 'nodes')  84.3 us
    dot_general x6, matrix products, contract_rows(): lax.dot_general(left_rows, right_rows, (((0,), (0,)), ((), ())), preferre...  20.7 us
    ppermute x8, starting transfers between devices, aggregate_back(): lax.ppermute(outward[link * num_slots:(link + 1) * num_slots], 'nodes', s...  15.2 us
    scatter-add x2, other arithmetic, aggregate_back(): return inner_sum.at[send_idx.reshape(-1)].add(returned)  14.2 us
    unnamed x20, local copies, waits for them, and re-layouts  8.46 us
    dot_general x1, matrix products, aggregate(): jnp.dot(a_int, features, preferred_element_type=jnp.float32)  7.39 us
    ppermute x4, starting transfers between devices, halo_rows(): lax.ppermute(sent_rows[link], 'nodes', shift_pairs(axis_size, offset))  5.1 us
    gather x1, local copies, waits for them, and re-layouts, halo_rows(): sent_rows = jnp.take(features, send_idx, axis=0)  3.94 us
  transfers between devices with their start and end apart: 13, of which 1 were waited for; matrix products, arithmetic and copies ran while one was open for 25% of the time, Pallas kernels for 0%

profile of v1, /device:TPU:21, one launch (start us, length us, event | category | flops | bytes accessed | tf_op | source)
XLA Modules:
  0.0 188.0 jit_solution(17218601089790662522)
XLA Ops:
  7.2 0.0 copy-start
  7.2 0.1 all-reduce.3.cloned.1.call-start
  7.3 0.9 copy-done
  8.2 2.9 %convolution_convert_fusion.2 = bf16[1024,107]{0,1:T(8,128)(2,1)S(1)} fusion(bf16[2048,1024]{1,0:T(8,128)(2,1)} %param.9, bf16[2048,107]{0,1:T(8,128)(2,1)S(1)} %copy-done), kind=kOutput, calls=%fused_computation.12 | convolution fusion | flops 448900096 | bytes 4851712 | tf_op jit(solution)/shard_map/dot_general | solution.py:16
  11.1 0.7 fusion.20
  11.8 4.7 %collective-permute-start.4 = (bf16[256,107]{0,1:T(8,128)(2,1)}, bf16[256,107]{0,1:T(8,128)(2,1)}, u32[]{:S(2)}, u32[]{:S(2)}) collective-permute-start(bf16[256,107]{0,1:T(8,128)(2,1)} %get-tuple-element.21), channel_id=1, source_target_pairs={{0,15},{1,0},{2,1},{3,2},{4,3},{5,4},{6,5},{7,6},{8,7},{9,8},{10,9... | collective-permute-start | bytes 164360 | tf_op jit(solution)/shard_map/ppermute | solution.py:34
  16.4 3.8 %collective-permute-start.6 = (bf16[256,107]{0,1:T(8,128)(2,1)S(1)}, bf16[256,107]{0,1:T(8,128)(2,1)}, u32[]{:S(2)}, u32[]{:S(2)}) collective-permute-start(bf16[256,107]{0,1:T(8,128)(2,1)S(1)} %get-tuple-element.23), channel_id=1, source_target_pairs={{0,14},{1,15},{2,0},{3,1},{4,2},{5,3},{6,4},{7,5},{8,6},{9,7},{10,... | collective-permute-start | bytes 164360 | tf_op jit(solution)/shard_map/ppermute | solution.py:34
  20.2 1.4 collective-permute-start.5
  21.7 0.5 copy.14
  22.2 3.9 %gather_fusion = bf16[1024,200]{1,0:T(8,128)(2,1)S(1)} fusion(bf16[2048,200]{1,0:T(8,128)(2,1)S(1)} %copy.14, s32[1024]{0:T(1024)S(1)} %broadcast_clamp_fusion), kind=kCustom, calls=%fused_computation | custom fusion | bytes 823296 | tf_op jit(solution)/shard_map/jit(_take)/gather | solution.py:20
  26.1 0.2 broadcast_select_fusion
  26.3 0.7 slice_bitcast_fusion.3
  27.0 0.0 collective-permute-start
  27.0 5.8 %fusion.22 = f32[2048,107]{1,0:T(8,128)S(1)} fusion(bf16[2048,2048]{1,0:T(8,128)(2,1)} %param.8, bf16[2048,107]{0,1:T(8,128)(2,1)S(1)} %copy-done), kind=kOutput, calls=%fused_computation.46 | convolution fusion | flops 897581056 | bytes 9703424 | tf_op jit(solution)/shard_map/dot_general | solution.py:16
  32.8 7.4 %fusion.21 = f32[2048,200]{0,1:T(8,128)} fusion(bf16[2048,2048]{1,0:T(8,128)(2,1)} %param.8, bf16[2048,200]{0,1:T(8,128)(2,1)S(1)} %copy-done.2), kind=kOutput, calls=%fused_computation.45 | convolution fusion | flops 1677721600 | bytes 10846208 | tf_op jit(solution)/shard_map/dot_general | solution.py:27
  40.2 4.3 %collective-permute-start.3 = (bf16[256,200]{1,0:T(8,128)(2,1)S(1)}, bf16[256,200]{1,0:T(8,128)(2,1)S(1)}, u32[]{:S(2)}, u32[]{:S(2)}) collective-permute-start(bf16[256,200]{1,0:T(8,128)(2,1)S(1)} %get-tuple-element.14), channel_id=1, source_target_pairs={{0,14},{1,15},{2,0},{3,1},{4,2},{5,3},{6,4},{7,5},{8,6},{9,7},{10,... | collective-permute-start | bytes 307208 | tf_op jit(solution)/shard_map/ppermute | solution.py:21
  44.5 0.8 collective-permute-start.1
  45.3 0.9 maximum_convert_fusion.2
  46.3 0.2 copy.16
  46.5 6.8 %scatter_fusion = f32[2048,107]{1,0:T(8,128)S(1)} fusion(f32[2048,107]{1,0:T(8,128)S(1)} %fusion.22, s32[1024]{0:T(1024)S(1)} %bitcast.46, f32[1024,107]{1,0:T(8,128)S(1)} %copy.16), kind=kCustom, calls=%fused_computation.1 | custom fusion | flops 109568 | bytes 1318912 | tf_op jit(solution)/shard_map/scatter-add | solution.py:36
  53.3 0.0 copy-start.1
  53.3 0.1 fusion.18
  53.4 0.0 copy-start.3
  53.5 1.2 copy-done.1
  54.7 3.7 %fusion.1 = bf16[2048,200]{0,1:T(8,128)(2,1)S(1)} fusion(f32[2048,200]{0,1:T(8,128)S(1)} %copy-done.1, bf16[2048,1024]{1,0:T(8,128)(2,1)} %param.9, bf16[256,200]{1,0:T(8,128)(2,1)S(1)} %collective-permute-done.3, bf16[256,200]{1,0:T(8,128)(2,1)S(1)} %collective-permute-done.2, bf16[256,200]{1,0:T(8,128)(2,1)S(1)} %collective-permute-done.1, ...), kind=kOutput, calls=%fused_computation.8 | convolution fusion | flops 841318400 | bytes 7061504 | tf_op jit(solution)/shard_map/dot_general | solution.py:27
  58.4 0.8 maximum_convert_fusion
  59.2 0.0 copy-start.6
  59.2 1.1 fusion.3
  60.4 1.0 select_convert_fusion
  61.4 1.3 fusion.23
  62.7 0.8 convolution_convert_fusion
  63.5 0.7 slice_add_fusion
  64.3 3.2 %fusion.2 = bf16[1024,200]{0,1:T(8,128)(2,1)S(1)} fusion(bf16[2048,200]{0,1:T(8,128)(2,1)S(1)} %convolution_convert_fusion, bf16[2048,1024]{1,0:T(8,128)(2,1)} %param.9), kind=kOutput, calls=%fused_computation.11 | convolution fusion | flops 839065600 | bytes 5423104 | tf_op jit(solution)/shard_map/dot_general | solution.py:16
  67.5 2.3 %collective-permute-start.8 = (bf16[256,200]{0,1:T(8,128)(2,1)S(1)}, bf16[256,200]{0,1:T(8,128)(2,1)S(1)}, u32[]{:S(2)}, u32[]{:S(2)}) collective-permute-start(bf16[256,200]{0,1:T(8,128)(2,1)S(1)} %get-tuple-element.17), channel_id=1, source_target_pairs={{0,15},{1,0},{2,1},{3,2},{4,3},{5,4},{6,5},{7,6},{8,7},{9,8},{10,9... | collective-permute-start | bytes 307208 | tf_op jit(solution)/shard_map/ppermute | solution.py:34
  69.8 2.7 %collective-permute-start.10 = (bf16[256,200]{0,1:T(8,128)(2,1)S(1)}, bf16[256,200]{0,1:T(8,128)(2,1)S(1)}, u32[]{:S(2)}, u32[]{:S(2)}) collective-permute-start(bf16[256,200]{0,1:T(8,128)(2,1)S(1)} %get-tuple-element.19), channel_id=1, source_target_pairs={{0,14},{1,15},{2,0},{3,1},{4,2},{5,3},{6,4},{7,5},{8,6},{9,7},{10,... | collective-permute-start | bytes 307208 | tf_op jit(solution)/shard_map/ppermute | solution.py:34
  72.5 0.4 collective-permute-start.9
  72.9 0.1 all-reduce.3.cloned.1.call-update
  72.9 6.4 %convolution_bitcast_fusion = f32[2048,200]{0,1:T(8,128)} fusion(bf16[2048,200]{0,1:T(8,128)(2,1)S(1)} %convolution_convert_fusion, bf16[2048,2048]{1,0:T(8,128)(2,1)} %param.8), kind=kOutput, calls=%fused_computation.5 | convolution fusion | flops 1677721600 | bytes 10846208 | tf_op jit(solution)/shard_map/dot_general | solution.py:16
  79.3 1.8 copy.17
  81.2 0.0 copy-start.4
  81.2 0.6 copy-done.4
  81.9 1.1 maximum_convert_fusion.1
  83.0 1.3 copy.18
  84.3 7.4 %scatter_fusion.1 = f32[2048,200]{1,0:T(8,128)S(1)} fusion(f32[2048,200]{1,0:T(8,128)S(1)} %copy.17, s32[1024]{0:T(1024)S(1)} %bitcast.47, f32[1024,200]{1,0:T(8,128)} %copy.18), kind=kCustom, calls=%fused_computation.2 | custom fusion | flops 204800 | bytes 2461696 | tf_op jit(solution)/shard_map/scatter-add | solution.py:36
  91.7 1.7 copy.19
  93.4 84.3 %all-reduce.3.cloned.1.call-done = (f32[200,512]{1,0:T(8,128)}, f32[512,107]{0,1:T(8,128)}) async-done(((f32[200,512]{1,0:T(8,128)}, f32[512,107]{0,1:T(8,128)}), (f32[200,512]{1,0:T(8,128)}, f32[512,107]{0,1:T(8,128)})) %all-reduce.3.cloned.1.call-update) | async-done | bytes 628752 | tf_op jit(solution)/shard_map/psum | solution.py:58
  177.7 1.8 copy.27
  179.5 1.6 copy.28
  (28 shorter events, 0.1 us)
Async XLA Ops:
  7.2 1.0 copy-start
  7.2 14.4 %copy-start.5 = (s32[4,256]{1,0:T(4,128)S(1)}, s32[4,256]{1,0:T(4,128)}, u32[]{:S(2)}) copy-start(s32[4,256]{1,0:T(4,128)} %param.10) | copy-start | bytes 12292
  7.2 14.5 %copy-start.2 = (bf16[2048,200]{0,1:T(8,128)(2,1)S(1)}, bf16[2048,200]{0,1:T(8,128)(2,1)}, u32[]{:S(2)}) copy-start(bf16[2048,200]{0,1:T(8,128)(2,1)} %param.7) | copy-start | bytes 2457604
  7.2 170.5 %all-reduce.3.cloned.1.call-start = ((), (), s32[]{:S(2)}) async-start(), calls=%async_computation | async-start | bytes 1277952 | tf_op jit(solution)/shard_map/psum | solution.py:58
  11.8 28.4 %collective-permute-start.4 = (bf16[256,107]{0,1:T(8,128)(2,1)}, bf16[256,107]{0,1:T(8,128)(2,1)}, u32[]{:S(2)}, u32[]{:S(2)}) collective-permute-start(bf16[256,107]{0,1:T(8,128)(2,1)} %get-tuple-element.21), channel_id=1, source_target_pairs={{0,15},{1,0},{2,1},{3,2},{4,3},{5,4},{6,5},{7,6},{8,7},{9,8},{10,9... | collective-permute-start | bytes 164360 | tf_op jit(solution)/shard_map/ppermute | solution.py:34
  16.4 28.0 %collective-permute-start.7 = (bf16[256,107]{0,1:T(8,128)(2,1)S(1)}, bf16[256,107]{0,1:T(8,128)(2,1)}, u32[]{:S(2)}, u32[]{:S(2)}) collective-permute-start(bf16[256,107]{0,1:T(8,128)(2,1)S(1)} %get-tuple-element.22), channel_id=1, source_target_pairs={{0,2},{1,3},{2,4},{3,5},{4,6},{5,7},{6,8},{7,9},{8,10},{9,11},{10,... | collective-permute-start | bytes 164360 | tf_op jit(solution)/shard_map/ppermute | solution.py:34
  16.4 28.0 %collective-permute-start.6 = (bf16[256,107]{0,1:T(8,128)(2,1)S(1)}, bf16[256,107]{0,1:T(8,128)(2,1)}, u32[]{:S(2)}, u32[]{:S(2)}) collective-permute-start(bf16[256,107]{0,1:T(8,128)(2,1)S(1)} %get-tuple-element.23), channel_id=1, source_target_pairs={{0,14},{1,15},{2,0},{3,1},{4,2},{5,3},{6,4},{7,5},{8,6},{9,7},{10,... | collective-permute-start | bytes 164360 | tf_op jit(solution)/shard_map/ppermute | solution.py:34
  20.2 25.1 %collective-permute-start.5 = (bf16[256,107]{0,1:T(8,128)(2,1)}, bf16[256,107]{0,1:T(8,128)(2,1)}, u32[]{:S(2)}, u32[]{:S(2)}) collective-permute-start(bf16[256,107]{0,1:T(8,128)(2,1)} %get-tuple-element.24), channel_id=1, source_target_pairs={{0,1},{1,2},{2,3},{3,4},{4,5},{5,6},{6,7},{7,8},{8,9},{9,10},{10,1... | collective-permute-start | bytes 164360 | tf_op jit(solution)/shard_map/ppermute | solution.py:34
  27.0 26.4 %collective-permute-start = (bf16[256,200]{1,0:T(8,128)(2,1)}, bf16[256,200]{1,0:T(8,128)(2,1)S(1)}, u32[]{:S(2)}, u32[]{:S(2)}) collective-permute-start(bf16[256,200]{1,0:T(8,128)(2,1)} %get-tuple-element.13), channel_id=1, source_target_pairs={{0,1},{1,2},{2,3},{3,4},{4,5},{5,6},{6,7},{7,8},{8,9},{9,10},{10,1... | collective-permute-start | bytes 307208 | tf_op jit(solution)/shard_map/ppermute | solution.py:21
  40.2 13.2 %collective-permute-start.3 = (bf16[256,200]{1,0:T(8,128)(2,1)S(1)}, bf16[256,200]{1,0:T(8,128)(2,1)S(1)}, u32[]{:S(2)}, u32[]{:S(2)}) collective-permute-start(bf16[256,200]{1,0:T(8,128)(2,1)S(1)} %get-tuple-element.14), channel_id=1, source_target_pairs={{0,14},{1,15},{2,0},{3,1},{4,2},{5,3},{6,4},{7,5},{8,6},{9,7},{10,... | collective-permute-start | bytes 307208 | tf_op jit(solution)/shard_map/ppermute | solution.py:21
  44.5 9.0 %collective-permute-start.2 = (bf16[256,200]{1,0:T(8,128)(2,1)S(1)}, bf16[256,200]{1,0:T(8,128)(2,1)S(1)}, u32[]{:S(2)}, u32[]{:S(2)}) collective-permute-start(bf16[256,200]{1,0:T(8,128)(2,1)S(1)} %get-tuple-element.15), channel_id=1, source_target_pairs={{0,2},{1,3},{2,4},{3,5},{4,6},{5,7},{6,8},{7,9},{8,10},{9,11},{10,... | collective-permute-start | bytes 307208 | tf_op jit(solution)/shard_map/ppermute | solution.py:21
  44.5 9.0 %collective-permute-start.1 = (bf16[256,200]{1,0:T(8,128)(2,1)S(1)}, bf16[256,200]{1,0:T(8,128)(2,1)S(1)}, u32[]{:S(2)}, u32[]{:S(2)}) collective-permute-start(bf16[256,200]{1,0:T(8,128)(2,1)S(1)} %get-tuple-element.16), channel_id=1, source_target_pairs={{0,15},{1,0},{2,1},{3,2},{4,3},{5,4},{6,5},{7,6},{8,7},{9,8},{10,9... | collective-permute-start | bytes 307208 | tf_op jit(solution)/shard_map/ppermute | solution.py:21
  53.3 1.4 copy-start.1
  53.4 5.0 %copy-start.3 = (bf16[200,512]{1,0:T(8,128)(2,1)S(1)}, bf16[200,512]{1,0:T(8,128)(2,1)}, u32[]{:S(2)}) copy-start(bf16[200,512]{1,0:T(8,128)(2,1)} %param.11) | copy-start | bytes 614404
  59.2 1.1 copy-start.6
  67.5 13.7 %collective-permute-start.8 = (bf16[256,200]{0,1:T(8,128)(2,1)S(1)}, bf16[256,200]{0,1:T(8,128)(2,1)S(1)}, u32[]{:S(2)}, u32[]{:S(2)}) collective-permute-start(bf16[256,200]{0,1:T(8,128)(2,1)S(1)} %get-tuple-element.17), channel_id=1, source_target_pairs={{0,15},{1,0},{2,1},{3,2},{4,3},{5,4},{6,5},{7,6},{8,7},{9,8},{10,9... | collective-permute-start | bytes 307208 | tf_op jit(solution)/shard_map/ppermute | solution.py:34
  69.8 11.4 %collective-permute-start.11 = (bf16[256,200]{0,1:T(8,128)(2,1)S(1)}, bf16[256,200]{0,1:T(8,128)(2,1)}, u32[]{:S(2)}, u32[]{:S(2)}) collective-permute-start(bf16[256,200]{0,1:T(8,128)(2,1)S(1)} %get-tuple-element.18), channel_id=1, source_target_pairs={{0,2},{1,3},{2,4},{3,5},{4,6},{5,7},{6,8},{7,9},{8,10},{9,11},{10,... | collective-permute-start | bytes 307208 | tf_op jit(solution)/shard_map/ppermute | solution.py:34
  69.8 11.4 %collective-permute-start.10 = (bf16[256,200]{0,1:T(8,128)(2,1)S(1)}, bf16[256,200]{0,1:T(8,128)(2,1)S(1)}, u32[]{:S(2)}, u32[]{:S(2)}) collective-permute-start(bf16[256,200]{0,1:T(8,128)(2,1)S(1)} %get-tuple-element.19), channel_id=1, source_target_pairs={{0,14},{1,15},{2,0},{3,1},{4,2},{5,3},{6,4},{7,5},{8,6},{9,7},{10,... | collective-permute-start | bytes 307208 | tf_op jit(solution)/shard_map/ppermute | solution.py:34
  72.5 9.4 %collective-permute-start.9 = (bf16[256,200]{0,1:T(8,128)(2,1)S(1)}, bf16[256,200]{0,1:T(8,128)(2,1)}, u32[]{:S(2)}, u32[]{:S(2)}) collective-permute-start(bf16[256,200]{0,1:T(8,128)(2,1)S(1)} %get-tuple-element.20), channel_id=1, source_target_pairs={{0,1},{1,2},{2,3},{3,4},{4,5},{5,6},{6,7},{7,8},{8,9},{9,10},{10,1... | collective-permute-start | bytes 307208 | tf_op jit(solution)/shard_map/ppermute | solution.py:34
  81.2 0.6 copy-start.4
Sparse Core Ops, SparseCore 0:
  73.1 104.5 all-reduce.2

commit v2 on v0

v2 whole, which is shorter than its diff:
```python
import functools

import jax
import jax.numpy as jnp
from jax import lax
from jax.experimental import pallas as pl
from jax.experimental.pallas import tpu as pltpu
from jax.sharding import PartitionSpec as P

BF16, F32 = jnp.bfloat16, jnp.float32
MESH = pl.DeviceIdType.MESH
LANES = 128


def link_offsets(num_links):
    return [(link // 2 + 1) * (1 - 2 * (link % 2)) for link in range(num_links)]


def round_up(size, unit):
    return -(-size // unit) * unit


def dot(left, right):
    return jnp.dot(left, right, preferred_element_type=F32)


def pad_lanes(value, width):
    return jnp.concatenate([value, jnp.zeros((value.shape[0], width - value.shape[1]), value.dtype)], axis=1)


def pad_rows(value, height):
    return jnp.concatenate([value, jnp.zeros((height - value.shape[0], value.shape[1]), value.dtype)], axis=0)


def gcn_kernel(axis_size, names, *refs):
    r = dict(zip(names, refs, strict=True))
    feats_hbm, aint_hbm, ahalo_hbm, idx_hbm = r["feats_hbm"], r["aint_hbm"], r["ahalo_hbm"], r["idx_hbm"]
    feats, aint, ahalo, idx, w1, w2, g = (r[k] for k in ("feats", "aint", "ahalo", "idx", "w1", "w2", "g"))
    nodes, feat_in = feats.shape
    hidden, classes = w2.shape
    links, slots = idx.shape
    halo = links * slots
    offsets = link_offsets(links)
    feat_pad = r["featp"].shape[1]
    class_pad = r["gT"].shape[0]
    class_rows = r["precv"].shape[0]
    feat_rows = r["e0T"].shape[0]
    block = 512
    num_blocks = nodes // block
    me = lax.axis_index("nodes")
    chips = axis_size // 2
    core = me % 2
    sign = 1 - 2 * core
    chip = me // 2

    def at_offset(offset):
        return (me + offset + axis_size) % axis_size

    def remote(src, dst, send_sem, recv_sem, target):
        return pltpu.make_async_remote_copy(src_ref=src, dst_ref=dst, send_sem=send_sem, recv_sem=recv_sem, device_id={"nodes": target}, device_id_type=MESH)

    lsem = r["local_sem"]
    small = [(idx_hbm, idx), (feats_hbm, feats), (r["g_hbm"], g), (r["w1_hbm"], w1), (r["w2_hbm"], w2)]
    pairs = small + [(ahalo_hbm.at[:, pl.ds(k * slots, slots)], ahalo.at[:, pl.ds(k * slots, slots)]) for k in range(links)]
    pairs += [(aint_hbm.at[:, pl.ds(j * block, block)], aint.at[:, pl.ds(j * block, block)]) for j in range(num_blocks)]
    copies = [pltpu.make_async_copy(src, dst, lsem.at[i]) for i, (src, dst) in enumerate(pairs)]
    for copy in copies:
        copy.start()
    c_idx, c_feats, c_g, c_w1, c_w2 = copies[:5]
    c_ahalo, c_aint = copies[5:5 + links], copies[5 + links:]

    barrier = pltpu.get_barrier_semaphore()
    peers = [1, -1, 2, -2, 4, -4]
    for offset in peers:
        pl.semaphore_signal(barrier, inc=1, device_id={"nodes": at_offset(offset)}, device_id_type=MESH)

    c_idx.wait()
    sel = r["sel"]
    r["idxp"][...] = jnp.zeros(r["idxp"].shape, F32)
    r["idxp"][0:links, :] = idx[...].astype(F32)
    r["idxT"][...] = r["idxp"][...].T
    step = 64
    for k in range(links):
        def fill(i, carry, k=k):
            col = r["idxT"][pl.ds(pl.multiple_of(i * step, step), step), k:k + 1]
            lane = lax.broadcasted_iota(jnp.int32, (step, nodes), 1).astype(F32)
            row = pl.multiple_of(k * slots + i * step, step)
            sel[pl.ds(row, step), :] = jnp.where(lane == col, 1.0, 0.0).astype(BF16)
            return carry
        lax.fori_loop(0, slots // step, fill, 0)

    c_feats.wait()
    featp = r["featp"]
    for b in range(num_blocks):
        rows = pl.ds(b * block, block)
        featp[rows, :] = pad_lanes(feats[rows, :], feat_pad)
    hsends = []
    for k in (2, 3, 0, 1):
        rows = pl.ds(k * slots, slots)
        r["hsend"][k] = dot(sel[rows, :], featp[...]).astype(BF16)
        if not hsends:
            pl.semaphore_wait(barrier, len(peers))
        copy = remote(r["hsend"].at[k], r["hrecv"].at[rows], r["h_ssem"].at[k], r["h_rsem"].at[k], at_offset(offsets[k]))
        copy.start()
        hsends.append(copy)

    c_g.wait()
    gT, pT = r["gT"], r["pT"]
    for b in range(num_blocks):
        rows = pl.ds(b * block, block)
        gT[:, rows] = pad_lanes(g[rows, :].astype(F32), class_pad).T.astype(BF16)
    psends = []
    for k in (2, 3, 0, 1):
        cols = pl.ds(k * slots, slots)
        c_ahalo[k].wait()
        r["psend"][k] = dot(gT[...], ahalo[:, cols])[0:class_rows].astype(BF16)
        copy = remote(r["psend"].at[k], r["precv"].at[:, cols], r["p_ssem"].at[k], r["p_rsem"].at[k], at_offset(-offsets[k]))
        copy.start()
        psends.append(copy)
    for b in range(num_blocks):
        cols = pl.ds(b * block, block)
        c_aint[b].wait()
        pT[:, cols] = dot(gT[...], aint[:, cols])

    zf, zb, zT, h1T = r["zf"], r["zb"], r["zT"], r["h1T"]
    for b in range(num_blocks):
        rows = pl.ds(b * block, block)
        zf[rows, :] = dot(aint[rows, :], featp[...])
    c_w1.wait()
    c_w2.wait()
    w1p = r["w1p"]
    w1p[...] = pad_rows(w1[...], feat_rows)
    r["w1T"][...] = pad_rows(w1[...].astype(F32), feat_pad).T.astype(BF16)
    w2v = pad_lanes(w2[...], class_pad)
    r["w2p"][...] = jnp.concatenate([w2v, w2v], axis=1)
    for copy in hsends:
        copy.wait_recv()
    for b in range(num_blocks):
        rows = pl.ds(b * block, block)
        z = zf[rows, :] + dot(ahalo[rows, :], r["hrecv"][...])
        zb[rows, :] = z.astype(BF16)
        zT[:, rows] = z.T.astype(BF16)
    for b in range(num_blocks):
        cols = pl.ds(b * block, block)
        h1T[:, cols] = jnp.maximum(dot(r["w1T"][...], zT[:, cols]), 0.0).astype(BF16)

    for copy in psends:
        copy.wait_recv()
    pairT, pair = r["pairT"], r["pair"]
    for b in range(num_blocks):
        cols = pl.ds(b * block, block)
        total = pT[:, cols] + pad_rows(dot(r["precv"][...], sel[:, cols]), class_pad)
        high = total.astype(BF16)
        low = total - high.astype(F32)
        pairT[0:class_pad, cols] = high
        pairT[class_pad:2 * class_pad, cols] = low.astype(BF16)
        pair[cols, 0:class_pad] = total.T.astype(BF16)
        pair[cols, class_pad:2 * class_pad] = low.T.astype(BF16)

    part, full = r["part"], r["full"]
    rows2, rows1 = hidden // axis_size, part.shape[1] - hidden // axis_size
    lane_groups = hidden // LANES
    second = dot(h1T[...], pair[...])
    second = second[:, 0:class_pad] + second[:, class_pad:2 * class_pad]
    for q in range(axis_size):
        part[q, 0:rows2, :] = second[q * rows2:(q + 1) * rows2]
    fT = r["fT"]
    for b in range(num_blocks):
        cols = pl.ds(b * block, block)
        d1T = dot(r["w2p"][...], pairT[:, cols])
        fT[:, cols] = jnp.where(h1T[:, cols].astype(F32) > 0, d1T, 0.0).astype(BF16)
    first = dot(fT[...], zb[...]).T
    for q in range(axis_size):
        row, lane = (q // lane_groups) * rows1, (q % lane_groups) * LANES
        part[q, rows2:rows2 + rows1, :] = first[row:row + rows1, lane:lane + LANES]

    half = core * chips
    other = (1 - core) * chips
    arsem_s, arsem_r = r["ar_ssem"], r["ar_rsem"]
    started = []

    def send(slot, src, dst, target):
        copy = remote(src, dst, arsem_s.at[slot], arsem_r.at[slot], target)
        copy.start()
        started.append(copy)
        return copy

    def chip_at(distance):
        return (chip + distance * sign + 2 * chips) % chips

    def device_at(distance):
        return chip_at(distance) * 2 + core

    sibling = me + sign
    mine, arbuf = r["mine"], r["arbuf"]
    swap = send(0, part.at[pl.ds(other, chips)], r["swap"], sibling)

    e0T, gradT = r["e0T"], r["gradT"]
    for b in range(num_blocks):
        cols = pl.ds(b * block, block)
        e0T[:, cols] = dot(w1p[...], fT[:, cols]).astype(BF16)

    swap.wait_recv()
    mine[...] = part[pl.ds(half, chips)] + r["swap"][...]
    c_a1 = send(1, mine.at[chip_at(-3)], arbuf.at[0], device_at(-1))
    c_a2 = send(2, mine.at[chip_at(4)], arbuf.at[1], device_at(-2))
    c_b = send(3, mine.at[chip_at(3)], arbuf.at[2], device_at(1))
    c_dp = send(4, mine.at[chip_at(-1)], arbuf.at[3], device_at(-1))
    c_dm = send(5, mine.at[chip_at(1)], arbuf.at[4], device_at(1))

    esends = []
    for k in (2, 3, 0, 1):
        cols = pl.ds(k * slots, slots)
        r["esend"][k] = dot(e0T[...], ahalo[:, cols]).astype(BF16)
        copy = remote(r["esend"].at[k], r["erecv"].at[:, cols], r["e_ssem"].at[k], r["e_rsem"].at[k], at_offset(-offsets[k]))
        copy.start()
        esends.append(copy)
    for b in range(num_blocks):
        cols = pl.ds(b * block, block)
        gradT[:, cols] = dot(e0T[...], aint[:, cols])

    c_a1.wait_recv()
    c_a2.wait_recv()
    r["relay"][0] = mine[chip_at(-2)] + arbuf[0] + arbuf[1]
    c_ep = send(6, r["relay"].at[0], arbuf.at[5], device_at(-2))
    c_b.wait_recv()
    r["relay"][1] = mine[chip_at(2)] + arbuf[2]
    c_em = send(7, r["relay"].at[1], arbuf.at[6], device_at(2))

    for copy in esends:
        copy.wait_recv()
    ostage = r["ostage"]
    outs = []
    for b in range(num_blocks):
        cols = pl.ds(b * block, block)
        total = gradT[:, cols] + dot(r["erecv"][...], sel[:, cols])
        ostage[cols, :] = pad_rows(total, feat_pad).T[:, 0:feat_in]
        copy = pltpu.make_async_copy(ostage.at[cols], r["gf_hbm"].at[cols], r["out_sem"].at[b])
        copy.start()
        outs.append(copy)

    for copy in (c_dp, c_dm, c_ep, c_em):
        copy.wait_recv()
    own = half + chip
    full[own] = mine[chip] + arbuf[3] + arbuf[4] + arbuf[5] + arbuf[6]

    def spread(slot, distance, target):
        place = full.at[half + chip_at(distance)]
        return send(slot, place, place, target)

    g_p1 = spread(8, 0, device_at(-1))
    g_m1 = spread(9, 0, device_at(1))
    g_p2 = spread(10, 0, device_at(-2))
    g_m2 = spread(11, 0, device_at(2))
    to_sibling = [spread(15, 0, sibling)]
    g_p2.wait_recv()
    g_p3 = spread(12, 2, device_at(-1))
    g_p4 = spread(13, 2, device_at(-2))
    g_m2.wait_recv()
    g_m3 = spread(14, -2, device_at(1))
    to_sibling.append(spread(16, 2, sibling))
    to_sibling.append(spread(17, -2, sibling))
    g_p1.wait_recv()
    to_sibling.append(spread(18, 1, sibling))
    g_m1.wait_recv()
    to_sibling.append(spread(19, -1, sibling))
    g_p3.wait_recv()
    to_sibling.append(spread(20, 3, sibling))
    g_m3.wait_recv()
    to_sibling.append(spread(21, -3, sibling))
    g_p4.wait_recv()
    to_sibling.append(spread(22, 4, sibling))
    for copy in to_sibling:
        copy.wait_recv()
    for q in range(axis_size):
        r["dw2"][q * rows2:(q + 1) * rows2, :] = full[q, 0:rows2, 0:classes]
        row, lane = (q // lane_groups) * rows1, (q % lane_groups) * LANES
        count = min(rows1, feat_in - row)
        r["dw1"][row:row + count, lane:lane + LANES] = full[q, rows2:rows2 + count, :]
    for copy in started + hsends + psends + esends:
        copy.wait_send()
    for copy in outs:
        copy.wait()


def gcn_backward(axis_size, node_feats, a_int, a_halo, send_idx, w_first, w_second, grad_out):
    nodes, feat_in = node_feats.shape
    hidden, classes = w_second.shape
    links, slots = send_idx.shape
    halo = links * slots
    chips = axis_size // 2
    assert chips == 8 and links == 4
    feat_pad = round_up(feat_in, 2 * LANES)
    feat_rows = round_up(feat_in, 16)
    class_pad = round_up(classes, LANES)
    class_rows = round_up(classes, 16)
    rows2 = hidden // axis_size
    rows1 = round_up(-(-feat_in // (axis_size // (hidden // LANES))), 8)
    chunk = (rows2 + rows1, LANES)
    vmem, dma = pltpu.VMEM, pltpu.SemaphoreType.DMA
    scratch = dict(
        feats=vmem((nodes, feat_in), BF16), aint=vmem((nodes, nodes), BF16), ahalo=vmem((nodes, halo), BF16), idx=vmem((links, slots), jnp.int32),
        w1=vmem((feat_in, hidden), BF16), w2=vmem((hidden, classes), BF16), g=vmem((nodes, classes), BF16),
        featp=vmem((nodes, feat_pad), BF16), idxp=vmem((LANES, slots), F32), idxT=vmem((slots, LANES), F32), sel=vmem((halo, nodes), BF16),
        hsend=vmem((links, slots, feat_pad), BF16), hrecv=vmem((halo, feat_pad), BF16),
        gT=vmem((class_pad, nodes), BF16), pT=vmem((class_pad, nodes), F32), psend=vmem((links, class_rows, slots), BF16), precv=vmem((class_rows, halo), BF16),
        zf=vmem((nodes, feat_pad), F32), zb=vmem((nodes, feat_pad), BF16), zT=vmem((feat_pad, nodes), BF16),
        w1p=vmem((feat_rows, hidden), BF16), w1T=vmem((hidden, feat_pad), BF16), w2p=vmem((hidden, 2 * class_pad), BF16),
        h1T=vmem((hidden, nodes), BF16), fT=vmem((hidden, nodes), BF16), pairT=vmem((2 * class_pad, nodes), BF16), pair=vmem((nodes, 2 * class_pad), BF16),
        e0T=vmem((feat_rows, nodes), BF16), esend=vmem((links, feat_rows, slots), BF16), erecv=vmem((feat_rows, halo), BF16), gradT=vmem((feat_rows, nodes), F32),
        ostage=vmem((nodes, feat_in), F32),
        part=vmem((axis_size,) + chunk, F32), swap=vmem((chips,) + chunk, F32), mine=vmem((chips,) + chunk, F32), arbuf=vmem((7,) + chunk, F32), relay=vmem((2,) + chunk, F32), full=vmem((axis_size,) + chunk, F32),
        local_sem=dma((16,)), out_sem=dma((4,)), h_ssem=dma((links,)), h_rsem=dma((links,)), p_ssem=dma((links,)), p_rsem=dma((links,)), e_ssem=dma((links,)), e_rsem=dma((links,)), ar_ssem=dma((23,)), ar_rsem=dma((23,)))
    names = ["feats_hbm", "aint_hbm", "ahalo_hbm", "idx_hbm", "w1_hbm", "w2_hbm", "g_hbm", "dw1", "dw2", "gf_hbm"] + list(scratch)
    any_spec = pl.BlockSpec(memory_space=pl.ANY)
    vmem_spec = pl.BlockSpec(memory_space=pltpu.VMEM)
    return pl.pallas_call(
        functools.partial(gcn_kernel, axis_size, names),
        out_shape=(jax.ShapeDtypeStruct((feat_in, hidden), F32), jax.ShapeDtypeStruct((hidden, classes), F32), jax.ShapeDtypeStruct((nodes, feat_in), F32)),
        in_specs=[any_spec] * 7,
        out_specs=(vmem_spec, vmem_spec, any_spec),
        scratch_shapes=list(scratch.values()),
        compiler_params=pltpu.CompilerParams(collective_id=0, has_side_effects=True, vmem_limit_bytes=62 * 1024 * 1024),
    )(node_feats, a_int, a_halo, send_idx, w_first, w_second, grad_out)


def solution(mesh):
    axis_size = mesh.shape["nodes"]
    row_spec = P(("graph", "nodes"), None)
    replicated = P(None, None)
    part_spec = P("graph", None)
    step = functools.partial(gcn_backward, axis_size)
    return jax.shard_map(step, mesh=mesh, in_specs=(row_spec, row_spec, row_spec, row_spec, replicated, replicated, row_spec), out_specs=(part_spec, part_spec, row_spec), check_vma=False)
```

time: 225 us -> 60.2 us (0.27)
  waiting for transfers between devices: 82.2 us -> 0 us
  Pallas kernels: 0 us -> 48 us
  matrix products: 45.8 us -> 0 us
  other arithmetic: 26.1 us -> 0 us
  starting transfers between devices: 22.7 us -> 0 us
  local copies, waits for them, and re-layouts: 32.9 us -> 11.3 us
  between operations: 14.4 us -> 0.65 us
    psum x1 -> x0, waiting for transfers between devices: 82.1 us -> none  [device_step(): dw_first = lax.psum(contract_rows(z_first, grad_pre), 'nodes')]
    pallas_call x0 -> x1, Pallas kernels: none -> 48 us  [gcn_backward(): pl.pallas_call(functools.partial(gcn_kernel, axis_size, names), out_shape...]
    dot_general x12 -> x0, matrix products: 45.8 us -> none  [the longest x6 25 us: contract_rows(): lax.dot_general(left_rows, right_rows, (((0,), (0,)), ((), ())), preferre...]
    ppermute x16 -> x0, starting transfers between devices: 22.6 us -> none  [the longest x8 14.2 us: halo_rows(): lax.ppermute(sent_rows[link], 'nodes', shift_pairs(axis_size, offset))]
    scatter-add x2 -> x0, other arithmetic: 19.1 us -> none  [aggregate_back(): return inner_sum.at[send_idx.reshape(-1)].add(returned)]
    gather x2 -> x0, local copies, waits for them, and re-layouts: 9.02 us -> none  [halo_rows(): sent_rows = jnp.take(features, send_idx, axis=0)]
    dot_general x2 -> x0, local copies, waits for them, and re-layouts: 7.29 us -> none  [contract_rows(): lax.dot_general(left_rows, right_rows, (((0,), (0,)), ((), ())), preferre...]
    pallas_call x0 -> x2, local copies, waits for them, and re-layouts: none -> 4.6 us  [gcn_backward(): pl.pallas_call(functools.partial(gcn_kernel, axis_size, names), out_shape...]
  transfers between devices with their start and end apart: 17 -> 0, of which waited for: 1 -> 0; matrix products, arithmetic and copies ran while one was open for 41% -> 0% of each run, Pallas kernels for 0% -> 0%
where the time goes in v2:
time: 60.2 us; the launch traced here: 60 us
  Pallas kernels  48 us (80%)
  local copies, waits for them, and re-layouts  11.3 us (19%)
  between operations  0.65 us (1%)
    pallas_call x1, Pallas kernels, gcn_backward(): pl.pallas_call(functools.partial(gcn_kernel, axis_size, names), out_shape...  48 us
    unnamed x6, local copies, waits for them, and re-layouts  6.68 us
    pallas_call x2, local copies, waits for them, and re-layouts, gcn_backward(): pl.pallas_call(functools.partial(gcn_kernel, axis_size, names), out_shape...  4.6 us

profile of v2, /device:TPU:21, one launch (start us, length us, event | category | flops | bytes accessed | tf_op | source)
XLA Modules:
  0.0 60.0 jit_solution(15580062913618662370)
XLA Ops:
  0.6 1.7 %copy.11.refs_5_ = bf16[512,107]{1,0:T(8,128)(2,1)} copy(bf16[512,107]{0,1:T(8,128)(2,1)} %param.12) | data formatting | bytes 219136 | tf_op args[5]
  2.3 2.0 %copy.12.refs_6_ = bf16[2048,107]{1,0:T(8,128)(2,1)} copy(bf16[2048,107]{0,1:T(8,128)(2,1)} %param.13) | data formatting | bytes 876544 | tf_op args[6]
  4.3 2.2 %copy.10.refs_0_ = bf16[2048,200]{1,0:T(8,128)(2,1)} copy(bf16[2048,200]{0,1:T(8,128)(2,1)} %param.7) | data formatting | bytes 1638400 | tf_op args[0]
  6.6 48.0 %shard_map.94 = (f32[200,512]{1,0:T(8,128)}, f32[512,107]{1,0:T(8,128)}, f32[2048,200]{1,0:T(8,128)}) custom-call(bf16[2048,200]{1,0:T(8,128)(2,1)} %copy.10.refs_0_, bf16[2048,2048]{1,0:T(8,128)(2,1)} %refs_1_.1, bf16[2048,1024]{1,0:T(8,128)(2,1)} %refs_2_.1, s32[4,256]{1,0:T(4,128)} %refs_3_.1, bf16[200,512]{1,0:T(8,128)(2,1)} %refs_4_.1, ...), custom_call_target="tpu_custom_call" | custom-call | tf_op jit(solution)/shard_map/pallas_call | solution.py:317
  54.6 0.0 copy-start
  54.6 1.8 %copy.13 = f32[512,107]{0,1:T(8,128)} copy(f32[512,107]{1,0:T(8,128)} %get-tuple-element.4) | data formatting | bytes 438272 | tf_op jit(solution)/shard_map/pallas_call | solution.py:317
  56.4 2.8 %copy.14 = f32[2048,200]{0,1:T(8,128)} copy(f32[2048,200]{1,0:T(8,128)} %get-tuple-element.5) | data formatting | bytes 3276800 | tf_op jit(solution)/shard_map/pallas_call | solution.py:317
  59.2 0.0 copy-done
  59.2 0.8 %copy.16 = f32[200,512]{1,0:T(8,128)} copy(f32[200,512]{1,0:T(8,128)S(1)} %copy-done) | data formatting | bytes 819200
Async XLA Ops:
  54.6 4.6 %copy-start = (f32[200,512]{1,0:T(8,128)S(1)}, f32[200,512]{1,0:T(8,128)}, u32[]{:S(2)}) copy-start(f32[200,512]{1,0:T(8,128)} %get-tuple-element.9) | copy-start | bytes 1228804

commit v3 on v2

v3 whole, which is shorter than its diff:
```python
import functools

import jax
import jax.numpy as jnp
from jax import lax
from jax.experimental import pallas as pl
from jax.experimental.pallas import tpu as pltpu
from jax.sharding import PartitionSpec as P

BF16, F32 = jnp.bfloat16, jnp.float32
MESH = pl.DeviceIdType.MESH
LANES = 128
VMEM_MIB = 56


def link_offsets(num_links):
    return [(link // 2 + 1) * (1 - 2 * (link % 2)) for link in range(num_links)]


def round_up(size, unit):
    return -(-size // unit) * unit


def dot(left, right):
    return jnp.dot(left, right, preferred_element_type=F32)


def dot_lanes(left, right):
    return lax.dot_general(left, right, (((1,), (1,)), ((), ())), preferred_element_type=F32)


def pad_lanes(value, width):
    return jnp.concatenate([value, jnp.zeros((value.shape[0], width - value.shape[1]), value.dtype)], axis=1)


def pad_rows(value, height):
    return jnp.concatenate([value, jnp.zeros((height - value.shape[0], value.shape[1]), value.dtype)], axis=0)


def gcn_kernel(axis_size, names, *refs):
    r = dict(zip(names, refs, strict=True))
    featsT, aint, ahalo, idx, w1, w2T, gT = (r[k] for k in ("featsT", "aint", "ahalo", "idx", "w1", "w2T", "gT"))
    feat_in, nodes = featsT.shape
    classes, hidden = w2T.shape
    links, slots = idx.shape
    halo = links * slots
    offsets = link_offsets(links)
    feat_pad = r["featp"].shape[0]
    class_pad = r["pT"].shape[0]
    class_rows = r["precv"].shape[0]
    feat_rows = r["e0T"].shape[0]
    block = 512
    num_blocks = nodes // block
    me = lax.axis_index("nodes")
    chips = axis_size // 2
    core = me % 2
    sign = 1 - 2 * core
    chip = me // 2
    order = (2, 3, 0, 1)

    def at_offset(offset):
        return (me + offset + axis_size) % axis_size

    def remote(src, dst, send_sem, recv_sem, target):
        return pltpu.make_async_remote_copy(src_ref=src, dst_ref=dst, send_sem=send_sem, recv_sem=recv_sem, device_id={"nodes": target}, device_id_type=MESH)

    lsem = r["local_sem"]
    pairs = [(r["idx_hbm"], idx), (r["featsT_hbm"], featsT), (r["gT_hbm"], gT)]
    row_blocks = [pl.ds(b * block, block) for b in range(num_blocks)]
    pairs += [(r["ahalo_hbm"].at[rows], ahalo.at[rows]) for rows in row_blocks]
    pairs += [(r["w1_hbm"], w1), (r["w2T_hbm"], w2T)]
    pairs += [(r["aint_hbm"].at[rows], aint.at[rows]) for rows in row_blocks]
    copies = [pltpu.make_async_copy(src, dst, lsem.at[i]) for i, (src, dst) in enumerate(pairs)]
    for copy in copies:
        copy.start()
    c_idx, c_feats, c_g = copies[:3]
    c_ahalo, (c_w1, c_w2), c_aint = copies[3:3 + num_blocks], copies[3 + num_blocks:5 + num_blocks], copies[5 + num_blocks:]

    barrier = pltpu.get_barrier_semaphore()
    peers = [1, -1, 2, -2, 4, -4]
    for offset in peers:
        pl.semaphore_signal(barrier, inc=1, device_id={"nodes": at_offset(offset)}, device_id_type=MESH)
    for k in range(links):
        r["hrecv"][k, feat_rows:feat_pad, :] = jnp.zeros((feat_pad - feat_rows, slots), BF16)

    c_idx.wait()
    pick = r["pick"]
    sub = 16
    hsends = []
    for k in order:
        index = idx[k:k + 1, :]
        low = jnp.broadcast_to(index % sub, (sub, slots))
        high = jnp.broadcast_to((index // sub).astype(F32), (sub, slots)).astype(BF16)
        ones = jnp.where(lax.broadcasted_iota(jnp.int32, (sub, slots), 0) == low, 1.0, 0.0).astype(BF16)
        zeros = jnp.zeros((sub, slots), BF16)
        for m in range(nodes // sub):
            pick[k % 2, m * sub:(m + 1) * sub, :] = jnp.where(high == jnp.array(m, BF16), ones, zeros)
        if not hsends:
            c_feats.wait()
        r["hsend"][k] = pad_rows(dot(featsT[...], pick[k % 2]), feat_rows).astype(BF16)
        if not hsends:
            pl.semaphore_wait(barrier, len(peers))
        copy = remote(r["hsend"].at[k], r["hrecv"].at[k, pl.ds(0, feat_rows)], r["h_ssem"].at[k], r["h_rsem"].at[k], at_offset(offsets[k]))
        copy.start()
        hsends.append(copy)

    c_g.wait()
    for copy in c_ahalo:
        copy.wait()
    psends = []
    for k in order:
        cols = pl.ds(k * slots, slots)
        r["psend"][k] = pad_rows(dot(gT[...], ahalo[:, cols]), class_rows).astype(BF16)
        copy = remote(r["psend"].at[k], r["precv"].at[:, cols], r["p_ssem"].at[k], r["p_rsem"].at[k], at_offset(-offsets[k]))
        copy.start()
        psends.append(copy)

    sel = r["sel"]
    r["idxp"][...] = jnp.zeros(r["idxp"].shape, F32)
    r["idxp"][0:links, :] = idx[...].astype(F32)
    r["idxT"][...] = r["idxp"][...].T
    step = 64
    for k in range(links):
        def fill(i, carry, k=k):
            col = r["idxT"][pl.ds(pl.multiple_of(i * step, step), step), k:k + 1]
            tile = jnp.floor(col * (1.0 / LANES))
            lane = lax.broadcasted_iota(jnp.int32, (step, LANES), 1).astype(F32)
            ones = jnp.where(lane == col - tile * LANES, 1.0, 0.0).astype(BF16)
            tile = jnp.broadcast_to(tile, (step, LANES)).astype(BF16)
            row = pl.multiple_of(k * slots + i * step, step)
            for t in range(nodes // LANES):
                sel[pl.ds(row, step), t * LANES:(t + 1) * LANES] = jnp.where(tile == jnp.array(t, BF16), ones, jnp.zeros((step, LANES), BF16))
            return carry
        lax.fori_loop(0, slots // step, fill, 0)

    featp, pT = r["featp"], r["pT"]
    featp[...] = pad_rows(featsT[...], feat_pad)
    zf, zb, zT, h1T = r["zf"], r["zb"], r["zT"], r["h1T"]
    for b in range(num_blocks):
        rows = pl.ds(b * block, block)
        c_aint[b].wait()
        zf[rows, :] = dot_lanes(aint[rows, :], featp[...])
    c_w1.wait()
    c_w2.wait()
    w1p = r["w1p"]
    w1p[...] = pad_rows(w1[...], feat_rows)
    r["w1T"][...] = pad_rows(w1[...].astype(F32), feat_pad).T.astype(BF16)
    w2v = pad_rows(w2T[...].astype(F32), class_pad).T.astype(BF16)
    r["w2p"][...] = jnp.concatenate([w2v, w2v], axis=1)
    for b in range(num_blocks):
        cols = pl.ds(b * block, block)
        pT[:, cols] = pad_rows(dot(gT[...], aint[:, cols]), class_pad)

    for i, k in enumerate(order):
        cols = pl.ds(k * slots, slots)
        hsends[i].wait_recv()
        for b in range(num_blocks):
            rows = pl.ds(b * block, block)
            z = zf[rows, :] + dot_lanes(ahalo[rows, cols], r["hrecv"][k])
            if i < links - 1:
                zf[rows, :] = z
            else:
                zb[rows, :] = z.astype(BF16)
                zT[:, rows] = z.T.astype(BF16)
    for b in range(num_blocks):
        cols = pl.ds(b * block, block)
        h1T[:, cols] = jnp.maximum(dot(r["w1T"][...], zT[:, cols]), 0.0).astype(BF16)

    for copy in psends:
        copy.wait_recv()
    pairT, pair = r["pairT"], r["pair"]
    for b in range(num_blocks):
        cols = pl.ds(b * block, block)
        total = pT[:, cols] + pad_rows(dot(r["precv"][...], sel[:, cols]), class_pad)
        high = total.astype(BF16)
        low = total - high.astype(F32)
        pairT[0:class_pad, cols] = high
        pairT[class_pad:2 * class_pad, cols] = low.astype(BF16)
        pair[cols, 0:class_pad] = total.T.astype(BF16)
        pair[cols, class_pad:2 * class_pad] = low.T.astype(BF16)

    fT = r["fT"]
    for b in range(num_blocks):
        cols = pl.ds(b * block, block)
        d1T = dot(r["w2p"][...], pairT[:, cols])
        fT[:, cols] = jnp.where(h1T[:, cols].astype(F32) > 0, d1T, 0.0).astype(BF16)
    part, full = r["part"], r["full"]
    pieces, rows_piece = part.shape[0], part.shape[2]
    lane_groups = hidden // LANES
    second = dot(h1T[...], pair[...])
    second = (second[:, 0:class_pad] + second[:, class_pad:2 * class_pad]).T
    first = dot(fT[...], zb[...]).T

    def places():
        for q in range(axis_size):
            for p in range(pieces):
                row = ((q // lane_groups) * pieces + p) * rows_piece
                yield p, q, row, pl.ds((q % lane_groups) * LANES, LANES)

    for p, q, row, lane in places():
        lanes = slice(lane.start, lane.start + LANES)
        if row < feat_in:
            part[p, q] = first[row:row + rows_piece, lanes]
        else:
            part[p, q] = second[row - feat_in:row - feat_in + rows_piece, lanes]

    half = core * chips
    other = (1 - core) * chips
    arsem_s, arsem_r = r["ar_ssem"], r["ar_rsem"]
    started = []

    def send(piece, slot, src, dst, target):
        copy = remote(src, dst, arsem_s.at[piece, slot], arsem_r.at[piece, slot], target)
        copy.start()
        started.append(copy)
        return copy

    def chip_at(distance):
        return (chip + distance * sign + 2 * chips) % chips

    def device_at(distance):
        return chip_at(distance) * 2 + core

    sibling = me + sign
    mine, arbuf, relay = r["mine"], r["arbuf"], r["relay"]
    swap = [send(p, 0, part.at[p, pl.ds(other, chips)], r["swap"].at[p], sibling) for p in range(pieces)]

    e0T, gradT = r["e0T"], r["gradT"]
    for b in range(num_blocks):
        cols = pl.ds(b * block, block)
        e0T[:, cols] = dot(w1p[...], fT[:, cols]).astype(BF16)

    first_step = []
    for p in range(pieces):
        swap[p].wait_recv()
        mine[p] = part[p, pl.ds(half, chips)] + r["swap"][p]
        first_step.append([
            send(p, 1, mine.at[p, chip_at(-3)], arbuf.at[p, 0], device_at(-1)),
            send(p, 2, mine.at[p, chip_at(4)], arbuf.at[p, 1], device_at(-2)),
            send(p, 3, mine.at[p, chip_at(3)], arbuf.at[p, 2], device_at(1)),
            send(p, 4, mine.at[p, chip_at(-1)], arbuf.at[p, 3], device_at(-1)),
            send(p, 5, mine.at[p, chip_at(1)], arbuf.at[p, 4], device_at(1))])

    esends = []
    for k in order:
        cols = pl.ds(k * slots, slots)
        r["esend"][k] = dot(e0T[...], ahalo[:, cols]).astype(BF16)
        copy = remote(r["esend"].at[k], r["erecv"].at[:, cols], r["e_ssem"].at[k], r["e_rsem"].at[k], at_offset(-offsets[k]))
        copy.start()
        esends.append(copy)
    for b in range(num_blocks):
        cols = pl.ds(b * block, block)
        gradT[:, cols] = dot(e0T[...], aint[:, cols])

    second_step = []
    for p in range(pieces):
        c_a1, c_a2, c_b = first_step[p][:3]
        c_a1.wait_recv()
        c_a2.wait_recv()
        relay[p, 0] = mine[p, chip_at(-2)] + arbuf[p, 0] + arbuf[p, 1]
        c_ep = send(p, 6, relay.at[p, 0], arbuf.at[p, 5], device_at(-2))
        c_b.wait_recv()
        relay[p, 1] = mine[p, chip_at(2)] + arbuf[p, 2]
        c_em = send(p, 7, relay.at[p, 1], arbuf.at[p, 6], device_at(2))
        second_step.append([c_ep, c_em])

    for copy in esends:
        copy.wait_recv()
    for b in range(num_blocks):
        cols = pl.ds(b * block, block)
        total = gradT[:, cols] + dot(r["erecv"][...], sel[:, cols])
        r["gfT"][:, cols] = total[0:feat_in]

    spreads = []

    def spread(piece, slot, distance, target):
        place = full.at[piece, half + chip_at(distance)]
        return send(piece, slot, place, place, target)

    for p in range(pieces):
        for copy in first_step[p][3:] + second_step[p]:
            copy.wait_recv()
        full[p, half + chip] = mine[p, chip] + arbuf[p, 3] + arbuf[p, 4] + arbuf[p, 5] + arbuf[p, 6]
        spreads.append([spread(p, 10, 0, device_at(-2)), spread(p, 11, 0, device_at(2)), spread(p, 8, 0, device_at(-1)), spread(p, 9, 0, device_at(1)), spread(p, 15, 0, sibling)])
    lasts = []
    for p in range(pieces):
        g_p2, g_m2, g_p1, g_m1, to_sibling = spreads[p]
        g_p2.wait_recv()
        g_p4 = spread(p, 13, 2, device_at(-2))
        g_p3 = spread(p, 12, 2, device_at(-1))
        g_m2.wait_recv()
        g_m3 = spread(p, 14, -2, device_at(1))
        back = [to_sibling, spread(p, 16, 2, sibling), spread(p, 17, -2, sibling)]
        g_p1.wait_recv()
        back.append(spread(p, 18, 1, sibling))
        g_m1.wait_recv()
        back.append(spread(p, 19, -1, sibling))
        lasts.append([g_p3, g_m3, g_p4, back])
    for p in range(pieces):
        g_p3, g_m3, g_p4, back = lasts[p]
        g_p3.wait_recv()
        back.append(spread(p, 20, 3, sibling))
        g_m3.wait_recv()
        back.append(spread(p, 21, -3, sibling))
        g_p4.wait_recv()
        back.append(spread(p, 22, 4, sibling))
    for p in range(pieces):
        for copy in lasts[p][3]:
            copy.wait_recv()
    for p, q, row, lane in places():
        if row < feat_in:
            r["dw1"][row:row + rows_piece, lane] = full[p, q]
        else:
            row = row - feat_in
            count = min(rows_piece, classes - row)
            r["dw2T"][row:row + count, lane] = full[p, q, 0:count, :]
    for copy in started + hsends + psends + esends:
        copy.wait_send()


def gcn_backward(axis_size, node_feats, a_int, a_halo, send_idx, w_first, w_second, grad_out):
    nodes, feat_in = node_feats.shape
    hidden, classes = w_second.shape
    links, slots = send_idx.shape
    halo = links * slots
    chips = axis_size // 2
    pieces = 2
    feat_pad = round_up(feat_in, 2 * LANES)
    feat_rows = round_up(feat_in, 16)
    class_pad = round_up(classes, LANES)
    class_rows = round_up(classes, 16)
    row_groups = axis_size // (hidden // LANES)
    rows_piece = round_up(-(-(feat_in + classes) // (row_groups * pieces)), 8)
    assert chips == 8 and links == 4 and feat_in % rows_piece == 0 and classes <= row_groups * pieces * rows_piece - feat_in <= class_pad
    chunk = (rows_piece, LANES)
    vmem, dma = pltpu.VMEM, pltpu.SemaphoreType.DMA
    scratch = dict(
        featsT=vmem((feat_in, nodes), BF16), aint=vmem((nodes, nodes), BF16), ahalo=vmem((nodes, halo), BF16), idx=vmem((links, slots), jnp.int32),
        w1=vmem((feat_in, hidden), BF16), w2T=vmem((classes, hidden), BF16), gT=vmem((classes, nodes), BF16),
        featp=vmem((feat_pad, nodes), BF16), idxp=vmem((LANES, slots), F32), idxT=vmem((slots, LANES), F32), pick=vmem((2, nodes, slots), BF16), sel=vmem((halo, nodes), BF16),
        hsend=vmem((links, feat_rows, slots), BF16), hrecv=vmem((links, feat_pad, slots), BF16),
        pT=vmem((class_pad, nodes), F32), psend=vmem((links, class_rows, slots), BF16), precv=vmem((class_rows, halo), BF16),
        zf=vmem((nodes, feat_pad), F32), zb=vmem((nodes, feat_pad), BF16), zT=vmem((feat_pad, nodes), BF16),
        w1p=vmem((feat_rows, hidden), BF16), w1T=vmem((hidden, feat_pad), BF16), w2p=vmem((hidden, 2 * class_pad), BF16),
        h1T=vmem((hidden, nodes), BF16), fT=vmem((hidden, nodes), BF16), pairT=vmem((2 * class_pad, nodes), BF16), pair=vmem((nodes, 2 * class_pad), BF16),
        e0T=vmem((feat_rows, nodes), BF16), esend=vmem((links, feat_rows, slots), BF16), erecv=vmem((feat_rows, halo), BF16), gradT=vmem((feat_rows, nodes), F32),
        part=vmem((pieces, axis_size) + chunk, F32), swap=vmem((pieces, chips) + chunk, F32), mine=vmem((pieces, chips) + chunk, F32), arbuf=vmem((pieces, 7) + chunk, F32), relay=vmem((pieces, 2) + chunk, F32), full=vmem((pieces, axis_size) + chunk, F32),
        local_sem=dma((16,)), h_ssem=dma((links,)), h_rsem=dma((links,)), p_ssem=dma((links,)), p_rsem=dma((links,)), e_ssem=dma((links,)), e_rsem=dma((links,)), ar_ssem=dma((pieces, 23)), ar_rsem=dma((pieces, 23)))
    names = ["featsT_hbm", "aint_hbm", "ahalo_hbm", "idx_hbm", "w1_hbm", "w2T_hbm", "gT_hbm", "dw1", "dw2T", "gfT"] + list(scratch)
    any_spec = pl.BlockSpec(memory_space=pltpu.HBM)
    vmem_spec = pl.BlockSpec(memory_space=pltpu.VMEM)
    dw_first, dw_second, grad_feats = pl.pallas_call(
        functools.partial(gcn_kernel, axis_size, names),
        out_shape=(jax.ShapeDtypeStruct((feat_in, hidden), F32), jax.ShapeDtypeStruct((classes, hidden), F32), jax.ShapeDtypeStruct((feat_in, nodes), F32)),
        in_specs=[any_spec] * 7,
        out_specs=(vmem_spec, vmem_spec, vmem_spec),
        scratch_shapes=list(scratch.values()),
        compiler_params=pltpu.CompilerParams(collective_id=0, has_side_effects=True, vmem_limit_bytes=VMEM_MIB * 1024 * 1024),
    )(node_feats.T, a_int, a_halo, send_idx, w_first, w_second.T, grad_out.T)
    return dw_first, dw_second.T, grad_feats.T


def solution(mesh):
    axis_size = mesh.shape["nodes"]
    row_spec = P(("graph", "nodes"), None)
    replicated = P(None, None)
    part_spec = P("graph", None)
    step = functools.partial(gcn_backward, axis_size)
    return jax.shard_map(step, mesh=mesh, in_specs=(row_spec, row_spec, row_spec, row_spec, replicated, replicated, row_spec), out_specs=(part_spec, part_spec, row_spec), check_vma=False)
```

time: 60.2 us -> 56.5 us (0.939)
  local copies, waits for them, and re-layouts: 11.3 us -> 6.18 us
  Pallas kernels: 48 us -> 49.5 us
    pallas_call x2 -> x0, local copies, waits for them, and re-layouts: 4.6 us -> none  [gcn_backward(): pl.pallas_call(functools.partial(gcn_kernel, axis_size, names), out_shape...]
    pallas_call x1, Pallas kernels: 48 us -> 49.5 us  [gcn_backward(): pl.pallas_call(functools.partial(gcn_kernel, axis_size, names), out_shape...]
    unnamed x6 -> x3, local copies, waits for them, and re-layouts: 6.68 us -> 6.18 us
where the time goes in v3:
time: 56.5 us; the launch traced here: 56.3 us
  Pallas kernels  49.5 us (88%)
  local copies, waits for them, and re-layouts  6.18 us (11%)
  between operations  0.64 us (1%)
    pallas_call x1, Pallas kernels, gcn_backward(): pl.pallas_call(functools.partial(gcn_kernel, axis_size, names), out_shape...  49.5 us
    unnamed x3, local copies, waits for them, and re-layouts  6.18 us

profile of v3, /device:TPU:21, one launch (start us, length us, event | category | flops | bytes accessed | tf_op | source)
XLA Modules:
  0.0 56.3 jit_solution(1090015935891165856)
XLA Ops:
  0.6 49.5 %shard_map.94 = (f32[200,512]{1,0:T(8,128)}, f32[107,512]{1,0:T(8,128)}, f32[200,2048]{1,0:T(8,128)}) custom-call(bf16[200,2048]{1,0:T(8,128)(2,1)} %bitcast.6, bf16[2048,2048]{1,0:T(8,128)(2,1)} %refs_1_.1, bf16[2048,1024]{1,0:T(8,128)(2,1)} %refs_2_.1, s32[4,256]{1,0:T(4,128)} %refs_3_.1, bf16[200,512]{1,0:T(8,128)(2,1)} %refs_4_.1, ...), custom_call_target="tpu_custom_call" | custom-call | tf_op jit(solution)/shard_map/pallas_call | solution.py:352
  50.2 1.8 %copy.13 = f32[200,512]{1,0:T(8,128)} copy(f32[200,512]{1,0:T(8,128)} %get-tuple-element.12) | data formatting | bytes 819200
  51.9 1.6 %copy.14 = f32[512,107]{0,1:T(8,128)} copy(f32[512,107]{0,1:T(8,128)} %bitcast.8) | data formatting | bytes 438272
  53.6 2.8 %copy.15 = f32[2048,200]{0,1:T(8,128)} copy(f32[2048,200]{0,1:T(8,128)} %bitcast.5) | data formatting | bytes 3276800

commit v4 on v3

--- a/solution.py
+++ b/solution.py
@@ -10,7 +10,7 @@
 BF16, F32 = jnp.bfloat16, jnp.float32
 MESH = pl.DeviceIdType.MESH
 LANES = 128
-VMEM_MIB = 56
+VMEM_MIB = 50
 
 
 def link_offsets(num_links):
@@ -71,7 +71,7 @@
     pairs += [(r["w1_hbm"], w1), (r["w2T_hbm"], w2T)]
     pairs += [(r["aint_hbm"].at[rows], aint.at[rows]) for rows in row_blocks]
     copies = [pltpu.make_async_copy(src, dst, lsem.at[i]) for i, (src, dst) in enumerate(pairs)]
-    for copy in copies:
+    for copy in copies[:3]:
         copy.start()
     c_idx, c_feats, c_g = copies[:3]
     c_ahalo, (c_w1, c_w2), c_aint = copies[3:3 + num_blocks], copies[3 + num_blocks:5 + num_blocks], copies[5 + num_blocks:]
@@ -97,6 +97,8 @@
             pick[k % 2, m * sub:(m + 1) * sub, :] = jnp.where(high == jnp.array(m, BF16), ones, zeros)
         if not hsends:
             c_feats.wait()
+            for copy in copies[3:]:
+                copy.start()
         r["hsend"][k] = pad_rows(dot(featsT[...], pick[k % 2]), feat_rows).astype(BF16)
         if not hsends:
             pl.semaphore_wait(barrier, len(peers))
@@ -166,44 +168,26 @@
         cols = pl.ds(b * block, block)
         h1T[:, cols] = jnp.maximum(dot(r["w1T"][...], zT[:, cols]), 0.0).astype(BF16)
 
-    for copy in psends:
-        copy.wait_recv()
     pairT, pair = r["pairT"], r["pair"]
-    for b in range(num_blocks):
-        cols = pl.ds(b * block, block)
-        total = pT[:, cols] + pad_rows(dot(r["precv"][...], sel[:, cols]), class_pad)
-        high = total.astype(BF16)
-        low = total - high.astype(F32)
-        pairT[0:class_pad, cols] = high
-        pairT[class_pad:2 * class_pad, cols] = low.astype(BF16)
-        pair[cols, 0:class_pad] = total.T.astype(BF16)
-        pair[cols, class_pad:2 * class_pad] = low.T.astype(BF16)
-
-    fT = r["fT"]
-    for b in range(num_blocks):
-        cols = pl.ds(b * block, block)
-        d1T = dot(r["w2p"][...], pairT[:, cols])
-        fT[:, cols] = jnp.where(h1T[:, cols].astype(F32) > 0, d1T, 0.0).astype(BF16)
+    for i, k in enumerate(order):
+        slot = pl.ds(k * slots, slots)
+        psends[i].wait_recv()
+        for b in range(num_blocks):
+            cols = pl.ds(b * block, block)
+            total = pT[:, cols] + pad_rows(dot(r["precv"][:, slot], sel[slot, cols]), class_pad)
+            if i < links - 1:
+                pT[:, cols] = total
+            else:
+                high = total.astype(BF16)
+                low = total - high.astype(F32)
+                pairT[0:class_pad, cols] = high
+                pairT[class_pad:2 * class_pad, cols] = low.astype(BF16)
+                pair[cols, 0:class_pad] = total.T.astype(BF16)
+                pair[cols, class_pad:2 * class_pad] = low.T.astype(BF16)
+
     part, full = r["part"], r["full"]
-    pieces, rows_piece = part.shape[0], part.shape[2]
-    lane_groups = hidden // LANES
-    second = dot(h1T[...], pair[...])
-    second = (second[:, 0:class_pad] + second[:, class_pad:2 * class_pad]).T
-    first = dot(fT[...], zb[...]).T
-
-    def places():
-        for q in range(axis_size):
-            for p in range(pieces):
-                row = ((q // lane_groups) * pieces + p) * rows_piece
-                yield p, q, row, pl.ds((q % lane_groups) * LANES, LANES)
-
-    for p, q, row, lane in places():
-        lanes = slice(lane.start, lane.start + LANES)
-        if row < feat_in:
-            part[p, q] = first[row:row + rows_piece, lanes]
-        else:
-            part[p, q] = second[row - feat_in:row - feat_in + rows_piece, lanes]
-
+    pieces = piece_rows(feat_in, classes, hidden, axis_size)
+    places = tile_places(feat_in, classes, hidden, axis_size)
     half = core * chips
     other = (1 - core) * chips
     arsem_s, arsem_r = r["ar_ssem"], r["ar_rsem"]
@@ -221,48 +205,96 @@
     def device_at(distance):
         return chip_at(distance) * 2 + core
 
+    def rows_of(p):
+        return pl.ds(pieces[p][0], pieces[p][1])
+
     sibling = me + sign
     mine, arbuf, relay = r["mine"], r["arbuf"], r["relay"]
-    swap = [send(p, 0, part.at[p, pl.ds(other, chips)], r["swap"].at[p], sibling) for p in range(pieces)]
+    numbers = range(len(pieces))
+    swap, first_step, second_step = {}, {}, {}
+
+    def write_tiles(which, value):
+        for q, row, owner, tile_row, lane in places:
+            if owner == which:
+                part[q, row:row + 8, :] = value[tile_row:tile_row + 8, lane:lane + LANES]
+
+    def start_swap(p):
+        swap[p] = send(p, 0, part.at[pl.ds(other, chips), rows_of(p)], r["swap"].at[:, rows_of(p)], sibling)
+
+    def start_first(p):
+        rows = rows_of(p)
+        swap[p].wait_recv()
+        mine[:, rows, :] = part[pl.ds(half, chips), rows, :] + r["swap"][:, rows, :]
+        first_step[p] = [
+            send(p, 2, mine.at[chip_at(4), rows], arbuf.at[1, rows], device_at(-2)),
+            send(p, 1, mine.at[chip_at(-3), rows], arbuf.at[0, rows], device_at(-1)),
+            send(p, 3, mine.at[chip_at(3), rows], arbuf.at[2, rows], device_at(1)),
+            send(p, 4, mine.at[chip_at(-1), rows], arbuf.at[3, rows], device_at(-1)),
+            send(p, 5, mine.at[chip_at(1), rows], arbuf.at[4, rows], device_at(1))]
+
+    def start_second(p):
+        rows = rows_of(p)
+        c_a2, c_a1, c_b = first_step[p][:3]
+        c_b.wait_recv()
+        relay[1, rows, :] = mine[chip_at(2), rows, :] + arbuf[2, rows, :]
+        c_em = send(p, 7, relay.at[1, rows], arbuf.at[6, rows], device_at(2))
+        c_a1.wait_recv()
+        c_a2.wait_recv()
+        relay[0, rows, :] = mine[chip_at(-2), rows, :] + arbuf[0, rows, :] + arbuf[1, rows, :]
+        c_ep = send(p, 6, relay.at[0, rows], arbuf.at[5, rows], device_at(-2))
+        second_step[p] = [c_em, c_ep]
+
+    second = dot(h1T[...], pair[...])
+    second = (second[:, 0:class_pad] + second[:, class_pad:2 * class_pad]).T
+    write_tiles(1, second)
+    start_swap(0)
+    fT = r["fT"]
+    for b in range(num_blocks):
+        cols = pl.ds(b * block, block)
+        d1T = dot(r["w2p"][...], pairT[:, cols])
+        fT[:, cols] = jnp.where(h1T[:, cols].astype(F32) > 0, d1T, 0.0).astype(BF16)
+    start_first(0)
+    first = dot(fT[...], zb[...]).T
+    write_tiles(0, first)
+    for p in numbers[1:]:
+        start_swap(p)
 
     e0T, gradT = r["e0T"], r["gradT"]
     for b in range(num_blocks):
         cols = pl.ds(b * block, block)
         e0T[:, cols] = dot(w1p[...], fT[:, cols]).astype(BF16)
 
-    first_step = []
-    for p in range(pieces):
-        swap[p].wait_recv()
-        mine[p] = part[p, pl.ds(half, chips)] + r["swap"][p]
-        first_step.append([
-            send(p, 1, mine.at[p, chip_at(-3)], arbuf.at[p, 0], device_at(-1)),
-            send(p, 2, mine.at[p, chip_at(4)], arbuf.at[p, 1], device_at(-2)),
-            send(p, 3, mine.at[p, chip_at(3)], arbuf.at[p, 2], device_at(1)),
-            send(p, 4, mine.at[p, chip_at(-1)], arbuf.at[p, 3], device_at(-1)),
-            send(p, 5, mine.at[p, chip_at(1)], arbuf.at[p, 4], device_at(1))])
-
     esends = []
-    for k in order:
+    for i, k in enumerate(order):
         cols = pl.ds(k * slots, slots)
         r["esend"][k] = dot(e0T[...], ahalo[:, cols]).astype(BF16)
+        if i == 0:
+            for p in numbers[1:]:
+                start_first(p)
         copy = remote(r["esend"].at[k], r["erecv"].at[:, cols], r["e_ssem"].at[k], r["e_rsem"].at[k], at_offset(-offsets[k]))
         copy.start()
         esends.append(copy)
+    start_second(0)
     for b in range(num_blocks):
         cols = pl.ds(b * block, block)
         gradT[:, cols] = dot(e0T[...], aint[:, cols])
-
-    second_step = []
-    for p in range(pieces):
-        c_a1, c_a2, c_b = first_step[p][:3]
-        c_a1.wait_recv()
-        c_a2.wait_recv()
-        relay[p, 0] = mine[p, chip_at(-2)] + arbuf[p, 0] + arbuf[p, 1]
-        c_ep = send(p, 6, relay.at[p, 0], arbuf.at[p, 5], device_at(-2))
-        c_b.wait_recv()
-        relay[p, 1] = mine[p, chip_at(2)] + arbuf[p, 2]
-        c_em = send(p, 7, relay.at[p, 1], arbuf.at[p, 6], device_at(2))
-        second_step.append([c_ep, c_em])
+    for p in numbers[1:]:
+        start_second(p)
+
+    spreads = {}
+
+    def spread(piece, slot, distance, target):
+        place = full.at[half + chip_at(distance), rows_of(piece)]
+        return send(piece, slot, place, place, target)
+
+    def start_spread(p):
+        rows = rows_of(p)
+        for copy in first_step[p][3:] + second_step[p]:
+            copy.wait_recv()
+        full[half + chip, rows, :] = mine[chip, rows, :] + arbuf[3, rows, :] + arbuf[4, rows, :] + arbuf[5, rows, :] + arbuf[6, rows, :]
+        spreads[p] = [spread(p, 10, 0, device_at(-2)), spread(p, 11, 0, device_at(2)), spread(p, 8, 0, device_at(-1)), spread(p, 9, 0, device_at(1)), spread(p, 15, 0, sibling)]
+
+    start_spread(0)
 
     for copy in esends:
         copy.wait_recv()
@@ -271,19 +303,10 @@
         total = gradT[:, cols] + dot(r["erecv"][...], sel[:, cols])
         r["gfT"][:, cols] = total[0:feat_in]
 
-    spreads = []
-
-    def spread(piece, slot, distance, target):
-        place = full.at[piece, half + chip_at(distance)]
-        return send(piece, slot, place, place, target)
-
-    for p in range(pieces):
-        for copy in first_step[p][3:] + second_step[p]:
-            copy.wait_recv()
-        full[p, half + chip] = mine[p, chip] + arbuf[p, 3] + arbuf[p, 4] + arbuf[p, 5] + arbuf[p, 6]
-        spreads.append([spread(p, 10, 0, device_at(-2)), spread(p, 11, 0, device_at(2)), spread(p, 8, 0, device_at(-1)), spread(p, 9, 0, device_at(1)), spread(p, 15, 0, sibling)])
+    for p in numbers[1:]:
+        start_spread(p)
     lasts = []
-    for p in range(pieces):
+    for p in numbers:
         g_p2, g_m2, g_p1, g_m1, to_sibling = spreads[p]
         g_p2.wait_recv()
         g_p4 = spread(p, 13, 2, device_at(-2))
@@ -296,7 +319,7 @@
         g_m1.wait_recv()
         back.append(spread(p, 19, -1, sibling))
         lasts.append([g_p3, g_m3, g_p4, back])
-    for p in range(pieces):
+    for p in numbers:
         g_p3, g_m3, g_p4, back = lasts[p]
         g_p3.wait_recv()
         back.append(spread(p, 20, 3, sibling))
@@ -304,18 +327,51 @@
         back.append(spread(p, 21, -3, sibling))
         g_p4.wait_recv()
         back.append(spread(p, 22, 4, sibling))
-    for p in range(pieces):
+    for p in numbers:
         for copy in lasts[p][3]:
             copy.wait_recv()
-    for p, q, row, lane in places():
-        if row < feat_in:
-            r["dw1"][row:row + rows_piece, lane] = full[p, q]
-        else:
-            row = row - feat_in
-            count = min(rows_piece, classes - row)
-            r["dw2T"][row:row + count, lane] = full[p, q, 0:count, :]
+    for q, row, owner, tile_row, lane in places:
+        if owner == 0:
+            r["dw1"][tile_row:tile_row + 8, lane:lane + LANES] = full[q, row:row + 8, :]
+        elif owner == 1:
+            count = min(8, classes - tile_row)
+            r["dw2T"][tile_row:tile_row + count, lane:lane + LANES] = full[q, row:row + count, :]
     for copy in started + hsends + psends + esends:
         copy.wait_send()
+
+
+def tile_counts(feat_in, classes, hidden, axis_size):
+    lane_groups = hidden // LANES
+    first, second = -(-feat_in // 8) * lane_groups, -(-classes // 8) * lane_groups
+    left = first % axis_size + second % axis_size
+    return second // axis_size, first // axis_size, -(-left // axis_size)
+
+
+def piece_rows(feat_in, classes, hidden, axis_size):
+    second, first, left = tile_counts(feat_in, classes, hidden, axis_size)
+    sizes = [8 * second, 8 * (first // 2), 8 * (first - first // 2 + left)]
+    return [(sum(sizes[:p]), size) for p, size in enumerate(sizes)]
+
+
+def tile_places(feat_in, classes, hidden, axis_size):
+    lane_groups = hidden // LANES
+    second, first, left = tile_counts(feat_in, classes, hidden, axis_size)
+    tiles = [[(owner, 8 * i, LANES * j) for i in range(-(-rows // 8)) for j in range(lane_groups)] for owner, rows in ((0, feat_in), (1, classes))]
+    rest = tiles[0][first * axis_size:] + tiles[1][second * axis_size:]
+    places = []
+    for base, count, group in ((0, second, tiles[1]), (second, first, tiles[0]), (second + first, left, rest)):
+        for i, tile in enumerate(group[:count * axis_size]):
+            places.append((i % axis_size, 8 * (base + i // axis_size)) + tile)
+    return places
+
+
+def store_kernel(*refs):
+    sources, targets, sems = refs[:3], refs[3:6], refs[6]
+    copies = [pltpu.make_async_copy(src, dst, sems.at[i]) for i, (src, dst) in enumerate(zip(sources, targets))]
+    for copy in copies:
+        copy.start()
+    for copy in copies:
+        copy.wait()
 
 
 def gcn_backward(axis_size, node_feats, a_int, a_halo, send_idx, w_first, w_second, grad_out):
@@ -324,15 +380,13 @@
     links, slots = send_idx.shape
     halo = links * slots
     chips = axis_size // 2
-    pieces = 2
     feat_pad = round_up(feat_in, 2 * LANES)
     feat_rows = round_up(feat_in, 16)
     class_pad = round_up(classes, LANES)
     class_rows = round_up(classes, 16)
-    row_groups = axis_size // (hidden // LANES)
-    rows_piece = round_up(-(-(feat_in + classes) // (row_groups * pieces)), 8)
-    assert chips == 8 and links == 4 and feat_in % rows_piece == 0 and classes <= row_groups * pieces * rows_piece - feat_in <= class_pad
-    chunk = (rows_piece, LANES)
+    pieces = piece_rows(feat_in, classes, hidden, axis_size)
+    assert chips == 8 and links == 4 and feat_in % 8 == 0
+    chunk = (pieces[-1][0] + pieces[-1][1], LANES)
     vmem, dma = pltpu.VMEM, pltpu.SemaphoreType.DMA
     scratch = dict(
         featsT=vmem((feat_in, nodes), BF16), aint=vmem((nodes, nodes), BF16), ahalo=vmem((nodes, halo), BF16), idx=vmem((links, slots), jnp.int32),
@@ -344,19 +398,27 @@
         w1p=vmem((feat_rows, hidden), BF16), w1T=vmem((hidden, feat_pad), BF16), w2p=vmem((hidden, 2 * class_pad), BF16),
         h1T=vmem((hidden, nodes), BF16), fT=vmem((hidden, nodes), BF16), pairT=vmem((2 * class_pad, nodes), BF16), pair=vmem((nodes, 2 * class_pad), BF16),
         e0T=vmem((feat_rows, nodes), BF16), esend=vmem((links, feat_rows, slots), BF16), erecv=vmem((feat_rows, halo), BF16), gradT=vmem((feat_rows, nodes), F32),
-        part=vmem((pieces, axis_size) + chunk, F32), swap=vmem((pieces, chips) + chunk, F32), mine=vmem((pieces, chips) + chunk, F32), arbuf=vmem((pieces, 7) + chunk, F32), relay=vmem((pieces, 2) + chunk, F32), full=vmem((pieces, axis_size) + chunk, F32),
-        local_sem=dma((16,)), h_ssem=dma((links,)), h_rsem=dma((links,)), p_ssem=dma((links,)), p_rsem=dma((links,)), e_ssem=dma((links,)), e_rsem=dma((links,)), ar_ssem=dma((pieces, 23)), ar_rsem=dma((pieces, 23)))
+        part=vmem((axis_size,) + chunk, F32), swap=vmem((chips,) + chunk, F32), mine=vmem((chips,) + chunk, F32), arbuf=vmem((7,) + chunk, F32), relay=vmem((2,) + chunk, F32), full=vmem((axis_size,) + chunk, F32),
+        local_sem=dma((16,)), h_ssem=dma((links,)), h_rsem=dma((links,)), p_ssem=dma((links,)), p_rsem=dma((links,)), e_ssem=dma((links,)), e_rsem=dma((links,)), ar_ssem=dma((len(pieces), 23)), ar_rsem=dma((len(pieces), 23)))
     names = ["featsT_hbm", "aint_hbm", "ahalo_hbm", "idx_hbm", "w1_hbm", "w2T_hbm", "gT_hbm", "dw1", "dw2T", "gfT"] + list(scratch)
     any_spec = pl.BlockSpec(memory_space=pltpu.HBM)
     vmem_spec = pl.BlockSpec(memory_space=pltpu.VMEM)
-    dw_first, dw_second, grad_feats = pl.pallas_call(
+    shapes = ((feat_in, hidden), (classes, hidden), (feat_in, nodes))
+    sums = pl.pallas_call(
         functools.partial(gcn_kernel, axis_size, names),
-        out_shape=(jax.ShapeDtypeStruct((feat_in, hidden), F32), jax.ShapeDtypeStruct((classes, hidden), F32), jax.ShapeDtypeStruct((feat_in, nodes), F32)),
+        out_shape=tuple(pltpu.VMEM(shape, F32) for shape in shapes),
         in_specs=[any_spec] * 7,
         out_specs=(vmem_spec, vmem_spec, vmem_spec),
         scratch_shapes=list(scratch.values()),
         compiler_params=pltpu.CompilerParams(collective_id=0, has_side_effects=True, vmem_limit_bytes=VMEM_MIB * 1024 * 1024),
-    )(node_feats.T, a_int, a_halo, send_idx, w_first, w_second.T, grad_out.T)
+    )(*[pltpu.with_memory_space_constraint(x, pltpu.HBM) for x in (node_feats.T, a_int, a_halo, send_idx, w_first, w_second.T, grad_out.T)])
+    dw_first, dw_second, grad_feats = pl.pallas_call(
+        store_kernel,
+        out_shape=tuple(jax.ShapeDtypeStruct(shape, F32) for shape in shapes),
+        in_specs=[vmem_spec] * 3,
+        out_specs=(any_spec,) * 3,
+        scratch_shapes=[dma((3,))],
+    )(*[pltpu.with_memory_space_constraint(x, pltpu.VMEM) for x in sums])
     return dw_first, dw_second.T, grad_feats.T
 
 

time: 56.5 us -> 52.8 us (0.935)
  local copies, waits for them, and re-layouts: 6.18 us -> 0 us
  Pallas kernels: 49.5 us -> 51.9 us
    unnamed x3 -> x0, local copies, waits for them, and re-layouts: 6.18 us -> none
    pallas_call x0 -> x1, Pallas kernels: none -> 1.4 us  [gcn_backward(): pl.pallas_call(store_kernel, out_shape=tuple((jax.ShapeDtypeStruct(shape,...]
    pallas_call x1, Pallas kernels: 49.5 us -> 50.5 us  [gcn_backward(): pl.pallas_call(functools.partial(gcn_kernel, axis_size, names), out_shape...]
where the time goes in v4:
time: 52.8 us; the launch traced here: 52.7 us
  Pallas kernels  51.9 us (98%)
  between operations  0.8 us (2%)
    pallas_call x1, Pallas kernels, gcn_backward(): pl.pallas_call(functools.partial(gcn_kernel, axis_size, names), out_shape...  50.5 us
    pallas_call x1, Pallas kernels, gcn_backward(): pl.pallas_call(store_kernel, out_shape=tuple((jax.ShapeDtypeStruct(shape,...  1.4 us

profile of v4, /device:TPU:21, one launch (start us, length us, event | category | flops | bytes accessed | tf_op | source)
XLA Modules:
  0.0 52.7 jit_solution(3787142279459331262)
XLA Ops:
  0.6 50.5 %shard_map.94 = (f32[200,512]{1,0:T(8,128)S(1)}, f32[107,512]{1,0:T(8,128)S(1)}, f32[200,2048]{1,0:T(8,128)S(1)}) custom-call(bf16[200,2048]{1,0:T(8,128)(2,1)} %bitcast.5, bf16[2048,2048]{1,0:T(8,128)(2,1)} %refs_1_.1, bf16[2048,1024]{1,0:T(8,128)(2,1)} %refs_2_.1, s32[4,256]{1,0:T(4,128)} %refs_3_.1, bf16[200,512]{1,0:T(8,128)(2,1)} %refs_4_.1, ...), custom_call_target="tpu_custom_call" | custom-call | tf_op jit(solution)/shard_map/pallas_call | solution.py:407
  51.1 1.4 %shard_map.95 = (f32[200,512]{1,0:T(8,128)}, f32[107,512]{1,0:T(8,128)}, f32[200,2048]{1,0:T(8,128)}) custom-call(f32[200,512]{1,0:T(8,128)S(1)} %get-tuple-element.9.refs_0_, f32[107,512]{1,0:T(8,128)S(1)} %get-tuple-element.10.refs_1_, f32[200,2048]{1,0:T(8,128)S(1)} %get-tuple-element.11.refs_2_), custom_call_target="tpu_custom_call" | custom-call | tf_op jit(solution)/shard_map/pallas_call | solution.py:415

commit v5 on v4

--- a/solution.py
+++ b/solution.py
@@ -71,77 +71,91 @@
     pairs += [(r["w1_hbm"], w1), (r["w2T_hbm"], w2T)]
     pairs += [(r["aint_hbm"].at[rows], aint.at[rows]) for rows in row_blocks]
     copies = [pltpu.make_async_copy(src, dst, lsem.at[i]) for i, (src, dst) in enumerate(pairs)]
-    for copy in copies[:3]:
+    for copy in copies[:5 + num_blocks]:
         copy.start()
     c_idx, c_feats, c_g = copies[:3]
     c_ahalo, (c_w1, c_w2), c_aint = copies[3:3 + num_blocks], copies[3 + num_blocks:5 + num_blocks], copies[5 + num_blocks:]
 
     barrier = pltpu.get_barrier_semaphore()
-    peers = [1, -1, 2, -2, 4, -4]
+    peers = [1, -1, 2, -2]
     for offset in peers:
         pl.semaphore_signal(barrier, inc=1, device_id={"nodes": at_offset(offset)}, device_id_type=MESH)
     for k in range(links):
         r["hrecv"][k, feat_rows:feat_pad, :] = jnp.zeros((feat_pad - feat_rows, slots), BF16)
 
     c_idx.wait()
-    pick = r["pick"]
+    pick, sel = r["pick"], r["sel"]
     sub = 16
-    hsends = []
-    for k in order:
+
+    def fill_pick(buffer, k):
         index = idx[k:k + 1, :]
         low = jnp.broadcast_to(index % sub, (sub, slots))
         high = jnp.broadcast_to((index // sub).astype(F32), (sub, slots)).astype(BF16)
         ones = jnp.where(lax.broadcasted_iota(jnp.int32, (sub, slots), 0) == low, 1.0, 0.0).astype(BF16)
         zeros = jnp.zeros((sub, slots), BF16)
+        cols = pl.ds((k % 2) * slots, slots)
         for m in range(nodes // sub):
-            pick[k % 2, m * sub:(m + 1) * sub, :] = jnp.where(high == jnp.array(m, BF16), ones, zeros)
-        if not hsends:
-            c_feats.wait()
-            for copy in copies[3:]:
-                copy.start()
-        r["hsend"][k] = pad_rows(dot(featsT[...], pick[k % 2]), feat_rows).astype(BF16)
-        if not hsends:
-            pl.semaphore_wait(barrier, len(peers))
-        copy = remote(r["hsend"].at[k], r["hrecv"].at[k, pl.ds(0, feat_rows)], r["h_ssem"].at[k], r["h_rsem"].at[k], at_offset(offsets[k]))
+            pick[buffer, m * sub:(m + 1) * sub, cols] = jnp.where(high == jnp.array(m, BF16), ones, zeros)
+
+    def fill_sel(k):
+        for i in range(slots // sub):
+            col = jnp.broadcast_to(r["idxT"][i * sub:(i + 1) * sub, k:k + 1], (sub, LANES))
+            tile = jnp.floor(col * (1.0 / LANES))
+            lane = lax.broadcasted_iota(jnp.int32, (sub, LANES), 1).astype(F32)
+            ones = jnp.where(lane == col - tile * LANES, 1.0, 0.0).astype(BF16)
+            tile = tile.astype(BF16)
+            row = k * slots + i * sub
+            for t in range(nodes // LANES):
+                sel[row:row + sub, t * LANES:(t + 1) * LANES] = jnp.where(tile == jnp.array(t, BF16), ones, jnp.zeros((sub, LANES), BF16))
+
+    def both(buffer, value, first):
+        buffer[first] = value[:, 0:slots]
+        buffer[first + 1] = value[:, slots:2 * slots]
+
+    hsends = {}
+
+    def send_rows(first):
+        for k in (first, first + 1):
+            hsends[k] = remote(r["hsend"].at[k], r["hrecv"].at[k, pl.ds(0, feat_rows)], r["h_ssem"].at[k], r["h_rsem"].at[k], at_offset(offsets[k]))
+            hsends[k].start()
+
+    fill_pick(0, 2)
+    fill_pick(0, 3)
+    c_feats.wait()
+    for copy in c_aint:
         copy.start()
-        hsends.append(copy)
+    both(r["hsend"], pad_rows(dot(featsT[...], pick[0]), feat_rows).astype(BF16), 2)
+    fill_pick(1, 0)
+    fill_pick(1, 1)
+    pl.semaphore_wait(barrier, len(peers))
+    send_rows(2)
+    both(r["hsend"], pad_rows(dot(featsT[...], pick[1]), feat_rows).astype(BF16), 0)
+    r["idxp"][...] = jnp.zeros(r["idxp"].shape, F32)
+    r["idxp"][0:links, :] = idx[...].astype(F32)
+    r["idxT"][...] = r["idxp"][...].T
+    send_rows(0)
 
     c_g.wait()
     for copy in c_ahalo:
         copy.wait()
-    psends = []
-    for k in order:
-        cols = pl.ds(k * slots, slots)
-        r["psend"][k] = pad_rows(dot(gT[...], ahalo[:, cols]), class_rows).astype(BF16)
-        copy = remote(r["psend"].at[k], r["precv"].at[:, cols], r["p_ssem"].at[k], r["p_rsem"].at[k], at_offset(-offsets[k]))
-        copy.start()
-        psends.append(copy)
-
-    sel = r["sel"]
-    r["idxp"][...] = jnp.zeros(r["idxp"].shape, F32)
-    r["idxp"][0:links, :] = idx[...].astype(F32)
-    r["idxT"][...] = r["idxp"][...].T
-    step = 64
-    for k in range(links):
-        def fill(i, carry, k=k):
-            col = r["idxT"][pl.ds(pl.multiple_of(i * step, step), step), k:k + 1]
-            tile = jnp.floor(col * (1.0 / LANES))
-            lane = lax.broadcasted_iota(jnp.int32, (step, LANES), 1).astype(F32)
-            ones = jnp.where(lane == col - tile * LANES, 1.0, 0.0).astype(BF16)
-            tile = jnp.broadcast_to(tile, (step, LANES)).astype(BF16)
-            row = pl.multiple_of(k * slots + i * step, step)
-            for t in range(nodes // LANES):
-                sel[pl.ds(row, step), t * LANES:(t + 1) * LANES] = jnp.where(tile == jnp.array(t, BF16), ones, jnp.zeros((step, LANES), BF16))
-            return carry
-        lax.fori_loop(0, slots // step, fill, 0)
+    psends = {}
+    for first in (2, 0):
+        both(r["psend"], pad_rows(dot(gT[...], ahalo[:, first * slots:(first + 2) * slots]), class_rows).astype(BF16), first)
+        fill_sel(first)
+        fill_sel(first + 1)
+        for k in (first, first + 1):
+            cols = pl.ds(k * slots, slots)
+            psends[k] = remote(r["psend"].at[k], r["precv"].at[:, cols], r["p_ssem"].at[k], r["p_rsem"].at[k], at_offset(-offsets[k]))
+            psends[k].start()
 
     featp, pT = r["featp"], r["pT"]
     featp[...] = pad_rows(featsT[...], feat_pad)
-    zf, zb, zT, h1T = r["zf"], r["zb"], r["zT"], r["h1T"]
-    for b in range(num_blocks):
-        rows = pl.ds(b * block, block)
+    zf, zT, h1T = r["zf"], r["zT"], r["h1T"]
+    for b in range(0, num_blocks, 2):
         c_aint[b].wait()
-        zf[rows, :] = dot_lanes(aint[rows, :], featp[...])
+        c_aint[b + 1].wait()
+        for rows in row_blocks[b:b + 2]:
+            zf[rows, :] = dot_lanes(aint[rows, :], featp[...])
     c_w1.wait()
     c_w2.wait()
     w1p = r["w1p"]
@@ -155,23 +169,22 @@
 
     for i, k in enumerate(order):
         cols = pl.ds(k * slots, slots)
-        hsends[i].wait_recv()
+        hsends[k].wait_recv()
         for b in range(num_blocks):
             rows = pl.ds(b * block, block)
             z = zf[rows, :] + dot_lanes(ahalo[rows, cols], r["hrecv"][k])
             if i < links - 1:
                 zf[rows, :] = z
             else:
-                zb[rows, :] = z.astype(BF16)
                 zT[:, rows] = z.T.astype(BF16)
     for b in range(num_blocks):
         cols = pl.ds(b * block, block)
         h1T[:, cols] = jnp.maximum(dot(r["w1T"][...], zT[:, cols]), 0.0).astype(BF16)
 
-    pairT, pair = r["pairT"], r["pair"]
+    pairT = r["pairT"]
     for i, k in enumerate(order):
         slot = pl.ds(k * slots, slots)
-        psends[i].wait_recv()
+        psends[k].wait_recv()
         for b in range(num_blocks):
             cols = pl.ds(b * block, block)
             total = pT[:, cols] + pad_rows(dot(r["precv"][:, slot], sel[slot, cols]), class_pad)
@@ -179,11 +192,8 @@
                 pT[:, cols] = total
             else:
                 high = total.astype(BF16)
-                low = total - high.astype(F32)
                 pairT[0:class_pad, cols] = high
-                pairT[class_pad:2 * class_pad, cols] = low.astype(BF16)
-                pair[cols, 0:class_pad] = total.T.astype(BF16)
-                pair[cols, class_pad:2 * class_pad] = low.T.astype(BF16)
+                pairT[class_pad:2 * class_pad, cols] = (total - high.astype(F32)).astype(BF16)
 
     part, full = r["part"], r["full"]
     pieces = piece_rows(feat_in, classes, hidden, axis_size)
@@ -244,19 +254,20 @@
         c_ep = send(p, 6, relay.at[0, rows], arbuf.at[5, rows], device_at(-2))
         second_step[p] = [c_em, c_ep]
 
-    second = dot(h1T[...], pair[...])
-    second = (second[:, 0:class_pad] + second[:, class_pad:2 * class_pad]).T
-    write_tiles(1, second)
-    start_swap(0)
     fT = r["fT"]
     for b in range(num_blocks):
         cols = pl.ds(b * block, block)
-        d1T = dot(r["w2p"][...], pairT[:, cols])
-        fT[:, cols] = jnp.where(h1T[:, cols].astype(F32) > 0, d1T, 0.0).astype(BF16)
-    start_first(0)
-    first = dot(fT[...], zb[...]).T
-    write_tiles(0, first)
-    for p in numbers[1:]:
+        d1T = dot(r["w2p"][...], pairT[:, cols]).astype(BF16)
+        fT[:, cols] = jnp.where(h1T[:, cols] > jnp.array(0, BF16), d1T, jnp.zeros_like(d1T))
+    second, first = [], []
+    for h in range(0, hidden, hidden // 2):
+        rows = pl.ds(h, hidden // 2)
+        value = dot_lanes(h1T[rows, :], pairT[...])
+        second.append((value[:, 0:class_pad] + value[:, class_pad:2 * class_pad]).T)
+        first.append(dot_lanes(fT[rows, :], zT[...]).T)
+    write_tiles(1, jnp.concatenate(second, axis=1))
+    write_tiles(0, jnp.concatenate(first, axis=1))
+    for p in numbers:
         start_swap(p)
 
     e0T, gradT = r["e0T"], r["gradT"]
@@ -264,22 +275,25 @@
         cols = pl.ds(b * block, block)
         e0T[:, cols] = dot(w1p[...], fT[:, cols]).astype(BF16)
 
-    esends = []
-    for i, k in enumerate(order):
-        cols = pl.ds(k * slots, slots)
-        r["esend"][k] = dot(e0T[...], ahalo[:, cols]).astype(BF16)
-        if i == 0:
-            for p in numbers[1:]:
-                start_first(p)
-        copy = remote(r["esend"].at[k], r["erecv"].at[:, cols], r["e_ssem"].at[k], r["e_rsem"].at[k], at_offset(-offsets[k]))
-        copy.start()
-        esends.append(copy)
-    start_second(0)
+    for p in numbers:
+        start_first(p)
+    for first in (2, 0):
+        both(r["esend"], dot(e0T[...], ahalo[:, first * slots:(first + 2) * slots]).astype(BF16), first)
+    esends = {}
+
+    def send_back(first):
+        for k in (first, first + 1):
+            cols = pl.ds(k * slots, slots)
+            esends[k] = remote(r["esend"].at[k], r["erecv"].at[:, cols], r["e_ssem"].at[k], r["e_rsem"].at[k], at_offset(-offsets[k]))
+            esends[k].start()
+
+    send_back(0)
     for b in range(num_blocks):
         cols = pl.ds(b * block, block)
         gradT[:, cols] = dot(e0T[...], aint[:, cols])
-    for p in numbers[1:]:
+    for p in numbers:
         start_second(p)
+    send_back(2)
 
     spreads = {}
 
@@ -294,17 +308,16 @@
         full[half + chip, rows, :] = mine[chip, rows, :] + arbuf[3, rows, :] + arbuf[4, rows, :] + arbuf[5, rows, :] + arbuf[6, rows, :]
         spreads[p] = [spread(p, 10, 0, device_at(-2)), spread(p, 11, 0, device_at(2)), spread(p, 8, 0, device_at(-1)), spread(p, 9, 0, device_at(1)), spread(p, 15, 0, sibling)]
 
-    start_spread(0)
-
-    for copy in esends:
+    for p in numbers:
+        start_spread(p)
+
+    for copy in esends.values():
         copy.wait_recv()
     for b in range(num_blocks):
         cols = pl.ds(b * block, block)
         total = gradT[:, cols] + dot(r["erecv"][...], sel[:, cols])
         r["gfT"][:, cols] = total[0:feat_in]
 
-    for p in numbers[1:]:
-        start_spread(p)
     lasts = []
     for p in numbers:
         g_p2, g_m2, g_p1, g_m1, to_sibling = spreads[p]
@@ -336,7 +349,7 @@
         elif owner == 1:
             count = min(8, classes - tile_row)
             r["dw2T"][tile_row:tile_row + count, lane:lane + LANES] = full[q, row:row + count, :]
-    for copy in started + hsends + psends + esends:
+    for copy in started + list(hsends.values()) + list(psends.values()) + list(esends.values()):
         copy.wait_send()
 
 
@@ -391,12 +404,12 @@
     scratch = dict(
         featsT=vmem((feat_in, nodes), BF16), aint=vmem((nodes, nodes), BF16), ahalo=vmem((nodes, halo), BF16), idx=vmem((links, slots), jnp.int32),
         w1=vmem((feat_in, hidden), BF16), w2T=vmem((classes, hidden), BF16), gT=vmem((classes, nodes), BF16),
-        featp=vmem((feat_pad, nodes), BF16), idxp=vmem((LANES, slots), F32), idxT=vmem((slots, LANES), F32), pick=vmem((2, nodes, slots), BF16), sel=vmem((halo, nodes), BF16),
+        featp=vmem((feat_pad, nodes), BF16), idxp=vmem((LANES, slots), F32), idxT=vmem((slots, LANES), F32), pick=vmem((2, nodes, 2 * slots), BF16), sel=vmem((halo, nodes), BF16),
         hsend=vmem((links, feat_rows, slots), BF16), hrecv=vmem((links, feat_pad, slots), BF16),
         pT=vmem((class_pad, nodes), F32), psend=vmem((links, class_rows, slots), BF16), precv=vmem((class_rows, halo), BF16),
-        zf=vmem((nodes, feat_pad), F32), zb=vmem((nodes, feat_pad), BF16), zT=vmem((feat_pad, nodes), BF16),
+        zf=vmem((nodes, feat_pad), F32), zT=vmem((feat_pad, nodes), BF16),
         w1p=vmem((feat_rows, hidden), BF16), w1T=vmem((hidden, feat_pad), BF16), w2p=vmem((hidden, 2 * class_pad), BF16),
-        h1T=vmem((hidden, nodes), BF16), fT=vmem((hidden, nodes), BF16), pairT=vmem((2 * class_pad, nodes), BF16), pair=vmem((nodes, 2 * class_pad), BF16),
+        h1T=vmem((hidden, nodes), BF16), fT=vmem((hidden, nodes), BF16), pairT=vmem((2 * class_pad, nodes), BF16),
         e0T=vmem((feat_rows, nodes), BF16), esend=vmem((links, feat_rows, slots), BF16), erecv=vmem((feat_rows, halo), BF16), gradT=vmem((feat_rows, nodes), F32),
         part=vmem((axis_size,) + chunk, F32), swap=vmem((chips,) + chunk, F32), mine=vmem((chips,) + chunk, F32), arbuf=vmem((7,) + chunk, F32), relay=vmem((2,) + chunk, F32), full=vmem((axis_size,) + chunk, F32),
         local_sem=dma((16,)), h_ssem=dma((links,)), h_rsem=dma((links,)), p_ssem=dma((links,)), p_rsem=dma((links,)), e_ssem=dma((links,)), e_rsem=dma((links,)), ar_ssem=dma((len(pieces), 23)), ar_rsem=dma((len(pieces), 23)))

time: 52.8 us -> 42.4 us (0.80)
  Pallas kernels: 51.9 us -> 41.5 us
    pallas_call x1, Pallas kernels: 50.5 us -> 40.1 us  [gcn_backward(): pl.pallas_call(functools.partial(gcn_kernel, axis_size, names), out_shape...]
where the time goes in v5:
time: 42.4 us; the launch traced here: 42.3 us
  Pallas kernels  41.5 us (98%)
  between operations  0.8 us (2%)
    pallas_call x1, Pallas kernels, gcn_backward(): pl.pallas_call(functools.partial(gcn_kernel, axis_size, names), out_shape...  40.1 us
    pallas_call x1, Pallas kernels, gcn_backward(): pl.pallas_call(store_kernel, out_shape=tuple((jax.ShapeDtypeStruct(shape,...  1.4 us

profile of v5, /device:TPU:21, one launch (start us, length us, event | category | flops | bytes accessed | tf_op | source)
XLA Modules:
  0.0 42.3 jit_solution(8419780991225618799)
XLA Ops:
  0.6 40.1 %shard_map.94 = (f32[200,512]{1,0:T(8,128)S(1)}, f32[107,512]{1,0:T(8,128)S(1)}, f32[200,2048]{1,0:T(8,128)S(1)}) custom-call(bf16[200,2048]{1,0:T(8,128)(2,1)} %bitcast.5, bf16[2048,2048]{1,0:T(8,128)(2,1)} %refs_1_.1, bf16[2048,1024]{1,0:T(8,128)(2,1)} %refs_2_.1, s32[4,256]{1,0:T(4,128)} %refs_3_.1, bf16[200,512]{1,0:T(8,128)(2,1)} %refs_4_.1, ...), custom_call_target="tpu_custom_call" | custom-call | tf_op jit(solution)/shard_map/pallas_call | solution.py:420
  40.7 1.4 %shard_map.95 = (f32[200,512]{1,0:T(8,128)}, f32[107,512]{1,0:T(8,128)}, f32[200,2048]{1,0:T(8,128)}) custom-call(f32[200,512]{1,0:T(8,128)S(1)} %get-tuple-element.9.refs_0_, f32[107,512]{1,0:T(8,128)S(1)} %get-tuple-element.10.refs_1_, f32[200,2048]{1,0:T(8,128)S(1)} %get-tuple-element.11.refs_2_), custom_call_target="tpu_custom_call" | custom-call | tf_op jit(solution)/shard_map/pallas_call | solution.py:428

commit v6 on v5

--- a/solution.py
+++ b/solution.py
@@ -80,8 +80,7 @@
     peers = [1, -1, 2, -2]
     for offset in peers:
         pl.semaphore_signal(barrier, inc=1, device_id={"nodes": at_offset(offset)}, device_id_type=MESH)
-    for k in range(links):
-        r["hrecv"][k, feat_rows:feat_pad, :] = jnp.zeros((feat_pad - feat_rows, slots), BF16)
+    r["hrecv"][feat_rows:feat_pad, :] = jnp.zeros((feat_pad - feat_rows, halo), BF16)
 
     c_idx.wait()
     pick, sel = r["pick"], r["sel"]
@@ -116,7 +115,7 @@
 
     def send_rows(first):
         for k in (first, first + 1):
-            hsends[k] = remote(r["hsend"].at[k], r["hrecv"].at[k, pl.ds(0, feat_rows)], r["h_ssem"].at[k], r["h_rsem"].at[k], at_offset(offsets[k]))
+            hsends[k] = remote(r["hsend"].at[k], r["hrecv"].at[pl.ds(0, feat_rows), pl.ds(k * slots, slots)], r["h_ssem"].at[k], r["h_rsem"].at[k], at_offset(offsets[k]))
             hsends[k].start()
 
     fill_pick(0, 2)
@@ -141,8 +140,6 @@
     psends = {}
     for first in (2, 0):
         both(r["psend"], pad_rows(dot(gT[...], ahalo[:, first * slots:(first + 2) * slots]), class_rows).astype(BF16), first)
-        fill_sel(first)
-        fill_sel(first + 1)
         for k in (first, first + 1):
             cols = pl.ds(k * slots, slots)
             psends[k] = remote(r["psend"].at[k], r["precv"].at[:, cols], r["p_ssem"].at[k], r["p_rsem"].at[k], at_offset(-offsets[k]))
@@ -156,6 +153,8 @@
         c_aint[b + 1].wait()
         for rows in row_blocks[b:b + 2]:
             zf[rows, :] = dot_lanes(aint[rows, :], featp[...])
+        fill_sel(b)
+        fill_sel(b + 1)
     c_w1.wait()
     c_w2.wait()
     w1p = r["w1p"]
@@ -167,13 +166,14 @@
         cols = pl.ds(b * block, block)
         pT[:, cols] = pad_rows(dot(gT[...], aint[:, cols]), class_pad)
 
-    for i, k in enumerate(order):
-        cols = pl.ds(k * slots, slots)
-        hsends[k].wait_recv()
+    for first in (2, 0):
+        cols = pl.ds(first * slots, 2 * slots)
+        for k in (first, first + 1):
+            hsends[k].wait_recv()
         for b in range(num_blocks):
             rows = pl.ds(b * block, block)
-            z = zf[rows, :] + dot_lanes(ahalo[rows, cols], r["hrecv"][k])
-            if i < links - 1:
+            z = zf[rows, :] + dot_lanes(ahalo[rows, cols], r["hrecv"][:, cols])
+            if first:
                 zf[rows, :] = z
             else:
                 zT[:, rows] = z.T.astype(BF16)
@@ -182,18 +182,14 @@
         h1T[:, cols] = jnp.maximum(dot(r["w1T"][...], zT[:, cols]), 0.0).astype(BF16)
 
     pairT = r["pairT"]
-    for i, k in enumerate(order):
-        slot = pl.ds(k * slots, slots)
+    for k in order:
         psends[k].wait_recv()
-        for b in range(num_blocks):
-            cols = pl.ds(b * block, block)
-            total = pT[:, cols] + pad_rows(dot(r["precv"][:, slot], sel[slot, cols]), class_pad)
-            if i < links - 1:
-                pT[:, cols] = total
-            else:
-                high = total.astype(BF16)
-                pairT[0:class_pad, cols] = high
-                pairT[class_pad:2 * class_pad, cols] = (total - high.astype(F32)).astype(BF16)
+    for b in range(num_blocks):
+        cols = pl.ds(b * block, block)
+        total = pT[:, cols] + pad_rows(dot(r["precv"][...], sel[:, cols]), class_pad)
+        high = total.astype(BF16)
+        pairT[0:class_pad, cols] = high
+        pairT[class_pad:2 * class_pad, cols] = (total - high.astype(F32)).astype(BF16)
 
     part, full = r["part"], r["full"]
     pieces = piece_rows(feat_in, classes, hidden, axis_size)
@@ -215,6 +211,9 @@
     def device_at(distance):
         return chip_at(distance) * 2 + core
 
+    def across(distance):
+        return chip_at(distance) * 2 + 1 - core
+
     def rows_of(p):
         return pl.ds(pieces[p][0], pieces[p][1])
 
@@ -223,10 +222,10 @@
     numbers = range(len(pieces))
     swap, first_step, second_step = {}, {}, {}
 
-    def write_tiles(which, value):
+    def write_tiles(which, value, lane0):
         for q, row, owner, tile_row, lane in places:
-            if owner == which:
-                part[q, row:row + 8, :] = value[tile_row:tile_row + 8, lane:lane + LANES]
+            if owner == which and lane0 <= lane < lane0 + value.shape[1]:
+                part[q, row:row + 8, :] = value[tile_row:tile_row + 8, lane - lane0:lane - lane0 + LANES]
 
     def start_swap(p):
         swap[p] = send(p, 0, part.at[pl.ds(other, chips), rows_of(p)], r["swap"].at[:, rows_of(p)], sibling)
@@ -255,27 +254,28 @@
         second_step[p] = [c_em, c_ep]
 
     fT = r["fT"]
-    for b in range(num_blocks):
-        cols = pl.ds(b * block, block)
-        d1T = dot(r["w2p"][...], pairT[:, cols]).astype(BF16)
-        fT[:, cols] = jnp.where(h1T[:, cols] > jnp.array(0, BF16), d1T, jnp.zeros_like(d1T))
-    second, first = [], []
-    for h in range(0, hidden, hidden // 2):
-        rows = pl.ds(h, hidden // 2)
+    for h in range(2):
+        rows = pl.ds(h * (hidden // 2), hidden // 2)
+        for b in range(num_blocks):
+            cols = pl.ds(b * block, block)
+            d1T = dot(r["w2p"][rows, :], pairT[:, cols]).astype(BF16)
+            fT[rows, cols] = jnp.where(h1T[rows, cols] > jnp.array(0, BF16), d1T, jnp.zeros_like(d1T))
         value = dot_lanes(h1T[rows, :], pairT[...])
-        second.append((value[:, 0:class_pad] + value[:, class_pad:2 * class_pad]).T)
-        first.append(dot_lanes(fT[rows, :], zT[...]).T)
-    write_tiles(1, jnp.concatenate(second, axis=1))
-    write_tiles(0, jnp.concatenate(first, axis=1))
-    for p in numbers:
-        start_swap(p)
+        write_tiles(1, (value[:, 0:class_pad] + value[:, class_pad:2 * class_pad]).T, h * (hidden // 2))
+        write_tiles(0, dot_lanes(fT[rows, :], zT[...]).T, h * (hidden // 2))
+        if h == 0:
+            start_swap(0)
+        else:
+            start_first(0)
+            for p in numbers[1:]:
+                start_swap(p)
 
     e0T, gradT = r["e0T"], r["gradT"]
     for b in range(num_blocks):
         cols = pl.ds(b * block, block)
         e0T[:, cols] = dot(w1p[...], fT[:, cols]).astype(BF16)
 
-    for p in numbers:
+    for p in numbers[1:]:
         start_first(p)
     for first in (2, 0):
         both(r["esend"], dot(e0T[...], ahalo[:, first * slots:(first + 2) * slots]).astype(BF16), first)
@@ -322,26 +322,17 @@
     for p in numbers:
         g_p2, g_m2, g_p1, g_m1, to_sibling = spreads[p]
         g_p2.wait_recv()
-        g_p4 = spread(p, 13, 2, device_at(-2))
-        g_p3 = spread(p, 12, 2, device_at(-1))
+        over = [spread(p, 13, 2, device_at(-2)), spread(p, 22, 2, across(-2)), spread(p, 12, 2, device_at(-1)), spread(p, 20, 2, across(-1))]
         g_m2.wait_recv()
-        g_m3 = spread(p, 14, -2, device_at(1))
+        over += [spread(p, 14, -2, device_at(1)), spread(p, 21, -2, across(1))]
         back = [to_sibling, spread(p, 16, 2, sibling), spread(p, 17, -2, sibling)]
         g_p1.wait_recv()
         back.append(spread(p, 18, 1, sibling))
         g_m1.wait_recv()
         back.append(spread(p, 19, -1, sibling))
-        lasts.append([g_p3, g_m3, g_p4, back])
+        lasts.append(back + over)
     for p in numbers:
-        g_p3, g_m3, g_p4, back = lasts[p]
-        g_p3.wait_recv()
-        back.append(spread(p, 20, 3, sibling))
-        g_m3.wait_recv()
-        back.append(spread(p, 21, -3, sibling))
-        g_p4.wait_recv()
-        back.append(spread(p, 22, 4, sibling))
-    for p in numbers:
-        for copy in lasts[p][3]:
+        for copy in lasts[p]:
             copy.wait_recv()
     for q, row, owner, tile_row, lane in places:
         if owner == 0:
@@ -353,28 +344,24 @@
         copy.wait_send()
 
 
-def tile_counts(feat_in, classes, hidden, axis_size):
-    lane_groups = hidden // LANES
-    first, second = -(-feat_in // 8) * lane_groups, -(-classes // 8) * lane_groups
-    left = first % axis_size + second % axis_size
-    return second // axis_size, first // axis_size, -(-left // axis_size)
+def tile_count(feat_in, classes, hidden, axis_size):
+    tiles = (-(-feat_in // 8) - (-classes // 8)) * (hidden // LANES // 2)
+    return -(-tiles // axis_size)
 
 
 def piece_rows(feat_in, classes, hidden, axis_size):
-    second, first, left = tile_counts(feat_in, classes, hidden, axis_size)
-    sizes = [8 * second, 8 * (first // 2), 8 * (first - first // 2 + left)]
+    count = tile_count(feat_in, classes, hidden, axis_size)
+    sizes = [8 * count, 8 * (count - count // 2), 8 * (count // 2)]
     return [(sum(sizes[:p]), size) for p, size in enumerate(sizes)]
 
 
 def tile_places(feat_in, classes, hidden, axis_size):
-    lane_groups = hidden // LANES
-    second, first, left = tile_counts(feat_in, classes, hidden, axis_size)
-    tiles = [[(owner, 8 * i, LANES * j) for i in range(-(-rows // 8)) for j in range(lane_groups)] for owner, rows in ((0, feat_in), (1, classes))]
-    rest = tiles[0][first * axis_size:] + tiles[1][second * axis_size:]
+    count = tile_count(feat_in, classes, hidden, axis_size)
+    groups = hidden // LANES // 2
     places = []
-    for base, count, group in ((0, second, tiles[1]), (second, first, tiles[0]), (second + first, left, rest)):
-        for i, tile in enumerate(group[:count * axis_size]):
-            places.append((i % axis_size, 8 * (base + i // axis_size)) + tile)
+    for h in range(2):
+        tiles = [(owner, 8 * i, LANES * (h * groups + j)) for owner, rows in ((1, classes), (0, feat_in)) for i in range(-(-rows // 8)) for j in range(groups)]
+        places += [(i % axis_size, 8 * (h * count + i // axis_size)) + tile for i, tile in enumerate(tiles)]
     return places
 
 
@@ -405,7 +392,7 @@
         featsT=vmem((feat_in, nodes), BF16), aint=vmem((nodes, nodes), BF16), ahalo=vmem((nodes, halo), BF16), idx=vmem((links, slots), jnp.int32),
         w1=vmem((feat_in, hidden), BF16), w2T=vmem((classes, hidden), BF16), gT=vmem((classes, nodes), BF16),
         featp=vmem((feat_pad, nodes), BF16), idxp=vmem((LANES, slots), F32), idxT=vmem((slots, LANES), F32), pick=vmem((2, nodes, 2 * slots), BF16), sel=vmem((halo, nodes), BF16),
-        hsend=vmem((links, feat_rows, slots), BF16), hrecv=vmem((links, feat_pad, slots), BF16),
+        hsend=vmem((links, feat_rows, slots), BF16), hrecv=vmem((feat_pad, halo), BF16),
         pT=vmem((class_pad, nodes), F32), psend=vmem((links, class_rows, slots), BF16), precv=vmem((class_rows, halo), BF16),
         zf=vmem((nodes, feat_pad), F32), zT=vmem((feat_pad, nodes), BF16),
         w1p=vmem((feat_rows, hidden), BF16), w1T=vmem((hidden, feat_pad), BF16), w2p=vmem((hidden, 2 * class_pad), BF16),

time: 42.4 us -> 41.9 us (0.988)
  no operation moved by 1% of the time
where the time goes in v6:
time: 41.9 us; the launch traced here: 41.8 us
  Pallas kernels  41.1 us (98%)
  between operations  0.64 us (2%)
    pallas_call x1, Pallas kernels, gcn_backward(): pl.pallas_call(functools.partial(gcn_kernel, axis_size, names), out_shape...  39.7 us
    pallas_call x1, Pallas kernels, gcn_backward(): pl.pallas_call(store_kernel, out_shape=tuple((jax.ShapeDtypeStruct(shape,...  1.4 us

profile of v6, /device:TPU:21, one launch (start us, length us, event | category | flops | bytes accessed | tf_op | source)
XLA Modules:
  0.0 41.8 jit_solution(3648972549418129813)
XLA Ops:
  0.6 39.7 %shard_map.94 = (f32[200,512]{1,0:T(8,128)S(1)}, f32[107,512]{1,0:T(8,128)S(1)}, f32[200,2048]{1,0:T(8,128)S(1)}) custom-call(bf16[200,2048]{1,0:T(8,128)(2,1)} %bitcast.5, bf16[2048,2048]{1,0:T(8,128)(2,1)} %refs_1_.1, bf16[2048,1024]{1,0:T(8,128)(2,1)} %refs_2_.1, s32[4,256]{1,0:T(4,128)} %refs_3_.1, bf16[200,512]{1,0:T(8,128)(2,1)} %refs_4_.1, ...), custom_call_target="tpu_custom_call" | custom-call | tf_op jit(solution)/shard_map/pallas_call | solution.py:407
  40.4 1.4 %shard_map.95 = (f32[200,512]{1,0:T(8,128)}, f32[107,512]{1,0:T(8,128)}, f32[200,2048]{1,0:T(8,128)}) custom-call(f32[200,512]{1,0:T(8,128)S(1)} %get-tuple-element.9.refs_0_, f32[107,512]{1,0:T(8,128)S(1)} %get-tuple-element.10.refs_1_, f32[200,2048]{1,0:T(8,128)S(1)} %get-tuple-element.11.refs_2_), custom_call_target="tpu_custom_call" | custom-call | tf_op jit(solution)/shard_map/pallas_call | solution.py:415
